TPU v7x, 32 devices: a whole 2x2x4 slice. The times are simulated.
32 devices in a mesh: lon: 8 (over y, x, core), lat: 4 (over z).
Axes of the slice: x: 2, y: 2, z: 4, core: 2. Of those that a mesh axis runs over, the one named last changes fastest.
Arguments:
- normed: bfloat16 [8, 96, 192, 192], P(None, 'lat', 'lon'), may hold values from -6 to 6
- cotangent: bfloat16 [8, 96, 192, 192], P(None, 'lat', 'lon'), may hold values from -6 to 6
- weight_qkv: bfloat16 [192, 576], replicated, may hold values from -0.4375 to 0.4375
- weight_proj: bfloat16 [192, 192], replicated, may hold values from -0.4375 to 0.4375
- bias_table: bfloat16 [64, 6, 20736], P('lat'), may hold values from -6 to 390
Outputs:
- input_grad: bfloat16 [8, 96, 192, 192], P(None, 'lat', 'lon')
- qkv_grad: float32 [192, 576], replicated
- proj_grad: float32 [192, 192], replicated
- bias_grad: float32 [64, 6, 20736], P('lat')
All inputs are finite; a program needn't handle non-finite values.
Results may differ from a plain program's by a relative error of at most 0.019.
Values may be sent and summed in bfloat16 or wider, within the bound.
A program may use at most 192 MiB of HBM per device.

v0:
```python
import jax
import jax.numpy as jnp
from jax import lax
from jax.sharding import PartitionSpec as P

HEADS = 6
WIN_Z = 2
WIN_LAT = 6
WIN_LON = 12
WTOK = 144


def from_behind(block, axis, distance):
    devices = range(lax.axis_size(axis))
    route = [((i - distance) % len(devices), i) for i in devices]
    return lax.ppermute(block, axis, route)


def passed_along(block, axis, distance):
    devices = range(lax.axis_size(axis))
    route = [(i - distance, i) for i in devices if i - distance in devices]
    return lax.ppermute(block, axis, route)


def window_split(grid_field):
    levels, height, breadth = grid_field.shape[:3]
    trailing_dims = grid_field.shape[3:]
    shaped = grid_field.reshape(
        (levels // WIN_Z, WIN_Z, height // WIN_LAT, WIN_LAT, breadth // WIN_LON, WIN_LON)
        + trailing_dims
    )
    axes_order = (0, 2, 4, 1, 3, 5) + tuple(range(6, 6 + len(trailing_dims)))
    return shaped.transpose(axes_order).reshape((-1, WTOK) + trailing_dims)


def window_merge(windowed, levels, height, breadth):
    channels = windowed.shape[-1]
    shaped = windowed.reshape(
        levels // WIN_Z, height // WIN_LAT, breadth // WIN_LON, WIN_Z, WIN_LAT, WIN_LON, channels
    )
    return shaped.transpose(0, 3, 1, 4, 2, 5, 6).reshape(levels, height, breadth, channels)


def window_backward(
    block_in, block_cot, block_region, block_live, block_types, bias_rows, weight_qkv, weight_proj
):
    windows = block_in.shape[0]
    channels = block_in.shape[2]
    head_dim = channels // HEADS
    softmax_scale = head_dim ** (-0.5)
    high = lax.Precision.HIGHEST
    f32 = jnp.float32
    projected = jnp.einsum("bnc,cf->bnf", block_in, weight_qkv, preferred_element_type=f32).astype(
        jnp.bfloat16
    )
    projected = projected.reshape(windows, WTOK, 3, HEADS, head_dim)
    queries = projected[:, :, 0]
    key_rows = projected[:, :, 1]
    values = projected[:, :, 2]
    bias_add = jnp.dot(
        block_types.astype(jnp.bfloat16), bias_rows, preferred_element_type=f32
    ).reshape(windows, HEADS, WTOK, WTOK)
    scores = (
        jnp.einsum("bqhd,bkhd->bhqk", queries, key_rows, preferred_element_type=f32) * softmax_scale
        + bias_add
    )
    allowed = (block_region[:, :, None] == block_region[:, None, :]) & (
        block_live[:, :, None] == block_live[:, None, :]
    )
    allowed = allowed[:, None]
    peak_score = jnp.max(jnp.where(allowed, scores, -1e30), axis=-1, keepdims=True)
    exp_terms = jnp.where(allowed, jnp.exp(scores - peak_score), 0.0)
    attn_probs = exp_terms / jnp.sum(exp_terms, axis=-1, keepdims=True)
    probs_b = attn_probs.astype(jnp.bfloat16)
    mixed = jnp.einsum("bhqk,bkhd->bqhd", probs_b, values, preferred_element_type=f32).astype(
        jnp.bfloat16
    )
    mixed = mixed.reshape(windows, WTOK, channels)
    grad_proj = jnp.einsum("bnc,bnf->cf", mixed, block_cot, preferred_element_type=f32)
    mixed_grad = jnp.einsum(
        "bnf,cf->bnc", block_cot, weight_proj, preferred_element_type=f32
    ).astype(jnp.bfloat16)
    mixed_grad = mixed_grad.reshape(windows, WTOK, HEADS, head_dim)
    prob_grad = jnp.einsum("bqhd,bkhd->bhqk", mixed_grad, values, preferred_element_type=f32)
    row_delta = jnp.sum(attn_probs * prob_grad, axis=-1, keepdims=True)
    score_grad = attn_probs * (prob_grad - row_delta)
    grad_bias = jnp.dot(
        block_types.T, score_grad.reshape(windows, -1), precision=high, preferred_element_type=f32
    )
    score_grad_b = score_grad.astype(jnp.bfloat16)
    query_grad = (
        jnp.einsum("bhqk,bkhd->bqhd", score_grad_b, key_rows, preferred_element_type=f32)
        * softmax_scale
    ).astype(jnp.bfloat16)
    key_grad = (
        jnp.einsum("bhqk,bqhd->bkhd", score_grad_b, queries, preferred_element_type=f32)
        * softmax_scale
    ).astype(jnp.bfloat16)
    value_grad = jnp.einsum(
        "bhqk,bqhd->bkhd", probs_b, mixed_grad, preferred_element_type=f32
    ).astype(jnp.bfloat16)
    cols_grad = jnp.stack([query_grad, key_grad, value_grad], axis=2).reshape(
        windows, WTOK, 3 * channels
    )
    grad_qkv = jnp.einsum("bnc,bnf->cf", block_in, cols_grad, preferred_element_type=f32)
    grad_in = jnp.einsum("bnf,cf->bnc", cols_grad, weight_qkv, preferred_element_type=f32).astype(
        jnp.bfloat16
    )
    return (grad_in, grad_qkv, grad_proj, grad_bias)


def local(normed, cotangent, weight_qkv, weight_proj, bias_table):
    levels, height, breadth, channels = normed.shape
    level_shift = WIN_Z // 2
    lat_shift = WIN_LAT // 2
    lon_shift = WIN_LON // 2
    normed = jnp.roll(normed, -level_shift, axis=0)
    cotangent = jnp.roll(cotangent, -level_shift, axis=0)
    across = from_behind((normed[:, :, :lon_shift], cotangent[:, :, :lon_shift]), "lon", -1)
    wide_in = jnp.concatenate([normed[:, :, lon_shift:], across[0]], axis=2)
    wide_cot = jnp.concatenate([cotangent[:, :, lon_shift:], across[1]], axis=2)
    upward = passed_along((wide_in[:, :lat_shift], wide_cot[:, :lat_shift]), "lat", -1)
    frame_in = jnp.concatenate([wide_in[:, lat_shift:], upward[0]], axis=1)
    frame_cot = jnp.concatenate([wide_cot[:, lat_shift:], upward[1]], axis=1)
    is_last = lax.axis_index("lat") == lax.axis_size("lat") - 1
    row_index = jnp.arange(height, dtype=jnp.int32)
    live_rows = jnp.logical_not(is_last & (row_index >= height - lat_shift))
    live_field = jnp.broadcast_to(live_rows[None, :, None], (levels, height, breadth))
    level_index = jnp.arange(levels, dtype=jnp.int32)
    wrapped_levels = (level_index >= levels - level_shift).astype(jnp.int32)
    wrapped_field = jnp.broadcast_to(wrapped_levels[:, None, None], (levels, height, breadth))
    level_windows = levels // WIN_Z
    lat_windows = height // WIN_LAT
    lon_windows = breadth // WIN_LON
    types_local = level_windows * lat_windows
    level_part = jnp.arange(level_windows, dtype=jnp.int32)[:, None, None]
    lat_part = jnp.arange(lat_windows, dtype=jnp.int32)[None, :, None]
    kinds = jnp.broadcast_to(
        lat_part * level_windows + level_part, (level_windows, lat_windows, lon_windows)
    )
    onehot = (
        kinds.reshape(-1)[:, None] == jnp.arange(types_local, dtype=jnp.int32)[None, :]
    ).astype(jnp.float32)
    bias_rows = bias_table.reshape(types_local, -1)
    framed_in = window_split(frame_in)
    window_total = framed_in.shape[0]
    block_size = max((divisor for divisor in range(1, 17) if window_total % divisor == 0))
    blocks = window_total // block_size

    def regroup(array):
        return array.reshape((blocks, block_size) + array.shape[1:])

    def step_block(totals, pieces):
        grad_in, grad_qkv, grad_proj, grad_bias = window_backward(
            pieces[0],
            pieces[1],
            pieces[2],
            pieces[3],
            pieces[4],
            bias_rows,
            weight_qkv,
            weight_proj,
        )
        return ((totals[0] + grad_qkv, totals[1] + grad_proj, totals[2] + grad_bias), grad_in)

    start = (
        jnp.zeros((channels, 3 * channels), jnp.float32),
        jnp.zeros((channels, channels), jnp.float32),
        jnp.zeros((types_local, HEADS * WTOK * WTOK), jnp.float32),
    )
    pieces = (
        regroup(framed_in),
        regroup(window_split(frame_cot)),
        regroup(window_split(wrapped_field)),
        regroup(window_split(live_field)),
        regroup(onehot),
    )
    totals, grads = lax.scan(step_block, start, pieces)
    framed_grad = window_merge(grads.reshape(window_total, WTOK, channels), levels, height, breadth)
    returned = passed_along(framed_grad[:, height - lat_shift :], "lat", 1)
    wide_grad = jnp.concatenate([returned, framed_grad[:, : height - lat_shift]], axis=1)
    sideways = from_behind(wide_grad[:, :, breadth - lon_shift :], "lon", 1)
    shifted_grad = jnp.concatenate([sideways, wide_grad[:, :, : breadth - lon_shift]], axis=2)
    input_grad = jnp.roll(shifted_grad, level_shift, axis=0)
    lat_qkv, lat_proj = (
        lax.psum(totals[0].astype(jnp.bfloat16), "lat").astype(jnp.float32),
        lax.psum(totals[1].astype(jnp.bfloat16), "lat").astype(jnp.float32),
    )
    bias_grad, qkv_grad, proj_grad = (
        lax.psum(totals[2].astype(jnp.bfloat16), "lon").astype(jnp.float32),
        lax.psum(lat_qkv.astype(jnp.bfloat16), "lon").astype(jnp.float32),
        lax.psum(lat_proj.astype(jnp.bfloat16), "lon").astype(jnp.float32),
    )
    return (input_grad, qkv_grad, proj_grad, bias_grad.reshape(types_local, HEADS, WTOK * WTOK))


def solution(mesh):
    in_specs = (
        P(None, "lat", "lon", None),
        P(None, "lat", "lon", None),
        P(),
        P(),
        P("lat", None, None),
    )
    out_specs = (P(None, "lat", "lon", None), P(), P(), P("lat", None, None))
    return jax.shard_map(local, mesh=mesh, in_specs=in_specs, out_specs=out_specs, check_vma=False)
```

profile of v0, /device:TPU:0, one launch (start us, length us, event | category | flops | bytes accessed | tf_op | source)
XLA Modules:
  0.0 629.4 jit_solution(3365991301374217343)
XLA Ops:
  68.9 396.9 %while.17 = (s32[]{:T(128)}, f32[192,576]{1,0:T(8,128)}, f32[192,192]{1,0:T(8,128)}, f32[16,124416]{1,0:T(8,128)}, bf16[2,16,144,192]{3,1,0,2:T(8,128)(2,1)}, /*...) while((s32[]{:T(128)}, f32[192,576]{1,0:T(8,128)}, ...), condition=%wide.region_4.5_spmd.clone, body=%wide.region_0.4_spmd.clone.sunk | while | flops 3127491072 | bytes 382142976 | solution.py:178
  72.4 15.1 %dot_general.59 = bf16[6,144,144,16]{2,1,0,3:T(8,128)(2,1)} reshape(bf16[124416,16]{0,1:T(8,128)(2,1)} %bitcast.192) | data formatting | bytes 7962624 | tf_op jit(solution)/shard_map/while/body/eval_jaxpr/dot_general | solution.py:60
  87.5 12.4 %fusion.128 = f32[16,6,144,144]{3,0,2,1:T(8,128)} fusion(bf16[6,144,144,16]{2,1,0,3:T(8,128)(2,1)} %dot_general.59, f32[2,16,16]{2,1,0:T(8,128)S(1)} %get-tuple-element.332, s32[]{:T(128)S(6)} %copy.169), kind=kOutput, calls=%fused_computation.8.clone.1 | convolution fusion | flops 63700992 | bytes 11948036 | tf_op jit(solution)/shard_map/while/body/eval_jaxpr/dot_general | solution.py:60
  99.8 17.0 %copy.157 = f32[16,6,144,144]{2,3,1,0:T(8,128)} copy(f32[16,6,144,144]{3,0,2,1:T(8,128)} %fusion.128) | data formatting | bytes 15925248 | tf_op jit(solution)/shard_map/while/body/eval_jaxpr/dot_general | solution.py:60
  124.3 13.1 %multiply_add_fusion.2 = f32[16,6,144,144]{2,3,1,0:T(8,128)} fusion(f32[16,6,144,144]{2,3,1,0:T(8,128)} %copy.157, bf16[16,144,3,6,32]{1,4,3,2,0:T(8,128)(2,1)} %bitcast.182), kind=kOutput, calls=%fused_computation.7.clone.1 | convolution fusion | flops 131383296 | bytes 25264128 | tf_op jit(solution)/shard_map/while/body/eval_jaxpr/bqhd,bkhd->bhqk/dot_general | solution.py:64
  138.5 15.3 %fusion.129 = (f32[16,6,144]{2,1,0:T(8,128)S(1)}, f32[16,6,144,144]{2,3,1,0:T(8,128)}) fusion(f32[16,6,144,144]{2,3,1,0:T(8,128)} %multiply_add_fusion.2, pred[16,144,144]{1,2,0:T(8,128)(4,1)S(1)} %compare_and_fusion.2), kind=kOutput, calls=%fused_computation.93.clone.1 | output fusion | flops 7962767 | bytes 16312320 | tf_op jit(solution)/shard_map/while/body/eval_jaxpr/sub | solution.py:72
  153.8 8.0 %fusion.130 = bf16[16,144,1,6,32]{1,4,3,0,2:T(8,128)(2,1)S(1)} fusion(bf16[16,144,6,32]{1,3,2,0:T(8,128)(2,1)} %bitcast.193, f32[16,6,144,144]{2,3,1,0:T(8,128)} %get-tuple-element.289, f32[16,6,144]{2,1,0:T(8,128)S(1)} %get-tuple-element.290), kind=kOutput, calls=%fused_computation.33.clone.1 | convolution fusion | flops 131825664 | bytes 9787392 | tf_op jit(solution)/shard_map/while/body/eval_jaxpr/bhqk,bqhd->bkhd/dot_general | solution.py:99
  163.4 9.7 %multiply_reduce_fusion.2 = (f32[16,6,144]{2,1,0:T(8,128)S(1)}, f32[16,6,144,144]{2,3,1,0:T(8,128)}) fusion(f32[16,6,144,144]{2,3,1,0:T(8,128)S(1)} %copy-done.1, f32[16,6,144]{2,1,0:T(8,128)S(1)} %get-tuple-element.290, bf16[16,144,6,32]{1,3,2,0:T(8,128)(2,1)} %bitcast.194, bf16[16,144,3,6,32]{1,4,3,2,0:T(8,128)(2,1)} %bitcast.183), kind=kOutput, calls=%fused_computation.3.clone.1 | convolution fusion | flops 133360128 | bytes 19181568 | tf_op jit(solution)/shard_map/while/body/eval_jaxpr/bqhd,bkhd->bhqk/dot_general | solution.py:84
  173.1 10.1 %subtract_multiply_fusion.2 = f32[16,6,144,144]{2,3,1,0:T(8,128)S(1)} fusion(f32[16,6,144,144]{2,3,1,0:T(8,128)} %get-tuple-element.291, f32[16,6,144]{2,1,0:T(8,128)S(1)} %get-tuple-element.292, f32[16,6,144,144]{2,3,1,0:T(8,128)} %get-tuple-element.289, f32[16,6,144]{2,1,0:T(8,128)S(1)} %get-tuple-element.290), kind=kLoop, calls=%fused_computation.2.clone.1 | loop fusion | flops 5971968 | bytes 23998464 | tf_op jit(solution)/shard_map/while/body/eval_jaxpr/mul | solution.py:86
  199.7 6.8 %fusion.134 = bf16[16,6,32,144]{3,2,1,0:T(8,128)(2,1)S(1)} fusion(bf16[16,144,3,6,32]{1,4,3,2,0:T(8,128)(2,1)} %bitcast.186, f32[16,6,144,144]{2,3,1,0:T(8,128)} %get-tuple-element.289, f32[16,6,144]{2,1,0:T(8,128)S(1)} %copy-done.8), kind=kOutput, calls=%fused_computation.27.clone.1 | convolution fusion | flops 131825664 | bytes 16668672 | tf_op jit(solution)/shard_map/while/body/eval_jaxpr/bhqk,bkhd->bqhd/dot_general | solution.py:75
  207.2 17.1 %copy.160 = f32[16,6,144,144]{3,2,1,0:T(8,128)} copy(f32[16,6,144,144]{2,3,1,0:T(8,128)} %copy-done) | data formatting | bytes 15925248 | tf_op jit(solution)/shard_map/while/body/eval_jaxpr/mul | solution.py:86
  224.3 23.2 %reshape.132 = f32[16,124416]{1,0:T(8,128)} reshape(f32[16,6,144,144]{3,2,1,0:T(8,128)} %copy.160) | data formatting | bytes 15925248 | tf_op jit(solution)/shard_map/while/body/eval_jaxpr/reshape | solution.py:88
  247.5 11.2 %convolution_add_fusion.2 = f32[16,124416]{1,0:T(8,128)} fusion(f32[16,124416]{1,0:T(8,128)} %reshape.132, f32[16,124416]{1,0:T(8,128)} %get-tuple-element.311, pred[]{:T(512)S(6)} %compare.3, f32[2,16,16]{2,1,0:T(8,128)S(1)} %get-tuple-element.332, s32[]{:T(128)S(6)} %copy.169), kind=kOutput, calls=%fused_computation.1.clone.1 | convolution fusion | flops 386187264 | bytes 23896068 | tf_op jit(solution)/shard_map/while/body/eval_jaxpr/dot_general | solution.py:87
  265.9 15.1 %dot_general.59 = bf16[6,144,144,16]{2,1,0,3:T(8,128)(2,1)} reshape(bf16[124416,16]{0,1:T(8,128)(2,1)} %bitcast.192) | data formatting | bytes 7962624 | tf_op jit(solution)/shard_map/while/body/eval_jaxpr/dot_general | solution.py:60
  281.0 12.4 %fusion.128 = f32[16,6,144,144]{3,0,2,1:T(8,128)} fusion(bf16[6,144,144,16]{2,1,0,3:T(8,128)(2,1)} %dot_general.59, f32[2,16,16]{2,1,0:T(8,128)S(1)} %get-tuple-element.332, s32[]{:T(128)S(6)} %copy.169), kind=kOutput, calls=%fused_computation.8.clone.1 | convolution fusion | flops 63700992 | bytes 11948036 | tf_op jit(solution)/shard_map/while/body/eval_jaxpr/dot_general | solution.py:60
  293.4 17.0 %copy.157 = f32[16,6,144,144]{2,3,1,0:T(8,128)} copy(f32[16,6,144,144]{3,0,2,1:T(8,128)} %fusion.128) | data formatting | bytes 15925248 | tf_op jit(solution)/shard_map/while/body/eval_jaxpr/dot_general | solution.py:60
  317.6 13.1 %multiply_add_fusion.2 = f32[16,6,144,144]{2,3,1,0:T(8,128)} fusion(f32[16,6,144,144]{2,3,1,0:T(8,128)} %copy.157, bf16[16,144,3,6,32]{1,4,3,2,0:T(8,128)(2,1)} %bitcast.182), kind=kOutput, calls=%fused_computation.7.clone.1 | convolution fusion | flops 131383296 | bytes 25264128 | tf_op jit(solution)/shard_map/while/body/eval_jaxpr/bqhd,bkhd->bhqk/dot_general | solution.py:64
  331.7 15.3 %fusion.129 = (f32[16,6,144]{2,1,0:T(8,128)S(1)}, f32[16,6,144,144]{2,3,1,0:T(8,128)}) fusion(f32[16,6,144,144]{2,3,1,0:T(8,128)} %multiply_add_fusion.2, pred[16,144,144]{1,2,0:T(8,128)(4,1)S(1)} %compare_and_fusion.2), kind=kOutput, calls=%fused_computation.93.clone.1 | output fusion | flops 7962767 | bytes 16312320 | tf_op jit(solution)/shard_map/while/body/eval_jaxpr/sub | solution.py:72
  347.1 8.0 %fusion.130 = bf16[16,144,1,6,32]{1,4,3,0,2:T(8,128)(2,1)S(1)} fusion(bf16[16,144,6,32]{1,3,2,0:T(8,128)(2,1)} %bitcast.193, f32[16,6,144,144]{2,3,1,0:T(8,128)} %get-tuple-element.289, f32[16,6,144]{2,1,0:T(8,128)S(1)} %get-tuple-element.290), kind=kOutput, calls=%fused_computation.33.clone.1 | convolution fusion | flops 131825664 | bytes 9787392 | tf_op jit(solution)/shard_map/while/body/eval_jaxpr/bhqk,bqhd->bkhd/dot_general | solution.py:99
  356.7 9.7 %multiply_reduce_fusion.2 = (f32[16,6,144]{2,1,0:T(8,128)S(1)}, f32[16,6,144,144]{2,3,1,0:T(8,128)}) fusion(f32[16,6,144,144]{2,3,1,0:T(8,128)S(1)} %copy-done.1, f32[16,6,144]{2,1,0:T(8,128)S(1)} %get-tuple-element.290, bf16[16,144,6,32]{1,3,2,0:T(8,128)(2,1)} %bitcast.194, bf16[16,144,3,6,32]{1,4,3,2,0:T(8,128)(2,1)} %bitcast.183), kind=kOutput, calls=%fused_computation.3.clone.1 | convolution fusion | flops 133360128 | bytes 19181568 | tf_op jit(solution)/shard_map/while/body/eval_jaxpr/bqhd,bkhd->bhqk/dot_general | solution.py:84
  366.3 10.1 %subtract_multiply_fusion.2 = f32[16,6,144,144]{2,3,1,0:T(8,128)S(1)} fusion(f32[16,6,144,144]{2,3,1,0:T(8,128)} %get-tuple-element.291, f32[16,6,144]{2,1,0:T(8,128)S(1)} %get-tuple-element.292, f32[16,6,144,144]{2,3,1,0:T(8,128)} %get-tuple-element.289, f32[16,6,144]{2,1,0:T(8,128)S(1)} %get-tuple-element.290), kind=kLoop, calls=%fused_computation.2.clone.1 | loop fusion | flops 5971968 | bytes 23998464 | tf_op jit(solution)/shard_map/while/body/eval_jaxpr/mul | solution.py:86
  393.1 6.8 %fusion.134 = bf16[16,6,32,144]{3,2,1,0:T(8,128)(2,1)S(1)} fusion(bf16[16,144,3,6,32]{1,4,3,2,0:T(8,128)(2,1)} %bitcast.186, f32[16,6,144,144]{2,3,1,0:T(8,128)} %get-tuple-element.289, f32[16,6,144]{2,1,0:T(8,128)S(1)} %copy-done.8), kind=kOutput, calls=%fused_computation.27.clone.1 | convolution fusion | flops 131825664 | bytes 16668672 | tf_op jit(solution)/shard_map/while/body/eval_jaxpr/bhqk,bkhd->bqhd/dot_general | solution.py:75
  400.5 17.1 %copy.160 = f32[16,6,144,144]{3,2,1,0:T(8,128)} copy(f32[16,6,144,144]{2,3,1,0:T(8,128)} %copy-done) | data formatting | bytes 15925248 | tf_op jit(solution)/shard_map/while/body/eval_jaxpr/mul | solution.py:86
  417.6 23.2 %reshape.132 = f32[16,124416]{1,0:T(8,128)} reshape(f32[16,6,144,144]{3,2,1,0:T(8,128)} %copy.160) | data formatting | bytes 15925248 | tf_op jit(solution)/shard_map/while/body/eval_jaxpr/reshape | solution.py:88
  440.8 13.3 %convolution_add_fusion.2 = f32[16,124416]{1,0:T(8,128)} fusion(f32[16,124416]{1,0:T(8,128)} %reshape.132, f32[16,124416]{1,0:T(8,128)} %get-tuple-element.311, pred[]{:T(512)S(6)} %compare.3, f32[2,16,16]{2,1,0:T(8,128)S(1)} %get-tuple-element.332, s32[]{:T(128)S(6)} %copy.169), kind=kOutput, calls=%fused_computation.1.clone.1 | convolution fusion | flops 386187264 | bytes 23896068 | tf_op jit(solution)/shard_map/while/body/eval_jaxpr/dot_general | solution.py:87
  469.2 5.5 convert_element_type.82
  474.8 9.0 %reshape.117 = bf16[16,6,20736]{2,1,0:T(8,128)(2,1)} reshape(bf16[16,124416]{1,0:T(8,128)(2,1)} %convert_element_type.82) | data formatting | bytes 7962624 | tf_op jit(solution)/shard_map/reshape | solution.py:194
  483.8 21.9 %all-reduce.7.cloned.1.call-done = (bf16[192,576]{1,0:T(8,128)(2,1)}, bf16[192,192]{1,0:T(8,128)(2,1)}) async-done(((bf16[192,576]{1,0:T(8,128)(2,1)}, bf16[192,192]{1,0:T(8,128)(2,1)}), (bf16[192,576]{1,0:T(8,128)(2,1)}, bf16[192,192]{1,0:T(8,128)(2,1)})) %all-reduce.7.cloned.1.call-update) | async-done | bytes 294928 | tf_op jit(solution)/shard_map/psum | solution.py:186
  514.5 5.2 reshape.116
  528.2 19.4 %collective-permute-done.5 = bf16[8,24,6,192]{3,0,2,1:T(8,128)(2,1)S(1)} collective-permute-done((bf16[8,24,6,192]{3,0,2,1:T(8,128)(2,1)S(1)}, bf16[8,24,6,192]{3,0,2,1:T(8,128)(2,1)S(1)}, u32[]{:S(2)}, u32[]{:S(2)}) %collective-permute-start.5) | collective-permute-done | bytes 442400 | tf_op jit(solution)/shard_map/ppermute | solution.py:16
  550.8 61.7 %all-reduce.5.cloned.1.call-done = (bf16[16,6,20736]{2,1,0:T(8,128)(2,1)}, bf16[192,576]{1,0:T(8,128)(2,1)}, bf16[192,192]{1,0:T(8,128)(2,1)}) async-done(((bf16[16,6,20736]{2,1,0:T(8,128)(2,1)}, bf16[192,576]{1,0:T(8,128)(2,1)}, bf16[192,192]{1,0:T(8,128)(2,1)}), (bf16[16,6,20736]{2,1,0:T(8,128)(2,1)}, bf16[192,576]{1,0:T(8,128)(2,1)}, bf16[192,192]{1,0:T(8,128)(2,1)})) %all-reduce.5.cloned.1.call-update) | async-done | bytes 4276240 | tf_op jit(solution)/shard_map/psum | solution.py:190
  615.8 6.5 %copy.117 = f32[16,6,20736]{2,0,1:T(8,128)} copy(bf16[16,6,20736]{2,1,0:T(8,128)(2,1)} %get-tuple-element.197) | data formatting | bytes 11943936
  (192 shorter events, 156.0 us)
Async XLA Ops:
  7.2 498.5 %all-reduce.7.cloned.1.call-start = ((), (), s32[]{:S(2)}) async-start(), calls=%async_computation.1 | async-start | bytes 688128 | tf_op jit(solution)/shard_map/psum | solution.py:186
  10.1 20.1 %collective-permute-start = (bf16[8,24,6,192]{3,1,2,0:T(8,128)(2,1)}, bf16[8,24,6,192]{3,1,2,0:T(8,128)(2,1)}, u32[]{:S(2)}, u32[]{:S(2)}) collective-permute-start(bf16[8,24,6,192]{3,1,2,0:T(8,128)(2,1)} %slice.92), channel_id=1, source_target_pairs={{4,0},{8,4},{12,8},{16,12},{20,16},{24,20},{28,24},{0,28},{5,1},{9... | collective-permute-start | bytes 1327112 | tf_op jit(solution)/shard_map/ppermute | solution.py:16
  16.8 15.9 %collective-permute-start.2 = (bf16[8,24,6,192]{3,1,2,0:T(8,128)(2,1)}, bf16[8,24,6,192]{3,1,2,0:T(8,128)(2,1)}, u32[]{:S(2)}, u32[]{:S(2)}) collective-permute-start(bf16[8,24,6,192]{3,1,2,0:T(8,128)(2,1)} %slice.96), channel_id=1, source_target_pairs={{4,0},{8,4},{12,8},{16,12},{20,16},{24,20},{28,24},{0,28},{5,1},{9... | collective-permute-start | bytes 1327112 | tf_op jit(solution)/shard_map/ppermute | solution.py:16
  31.4 11.8 %collective-permute-start.1 = (bf16[8,3,24,192]{3,2,1,0:T(8,128)(2,1)S(1)}, bf16[8,3,24,192]{3,2,1,0:T(8,128)(2,1)S(1)}, u32[]{:S(2)}, u32[]{:S(2)}) collective-permute-start(bf16[8,3,24,192]{3,2,1,0:T(8,128)(2,1)S(1)} %copy.101), channel_id=1, source_target_pairs={{1,0},{2,1},{3,2},{5,4},{6,5},{7,6},{9,8},{10,9},{11,10},{13,12},{... | collective-permute-start | bytes 663560 | tf_op jit(solution)/shard_map/ppermute | solution.py:22
  34.5 18.7 %collective-permute-start.3 = (bf16[8,3,24,192]{3,2,1,0:T(8,128)(2,1)}, bf16[8,3,24,192]{3,2,1,0:T(8,128)(2,1)}, u32[]{:S(2)}, u32[]{:S(2)}) collective-permute-start(bf16[8,3,24,192]{3,2,1,0:T(8,128)(2,1)} %copy.108), channel_id=1, source_target_pairs={{1,0},{2,1},{3,2},{5,4},{6,5},{7,6},{9,8},{10,9},{11,10},{13,12},{... | collective-permute-start | bytes 663560 | tf_op jit(solution)/shard_map/ppermute | solution.py:22
  69.2 18.3 %copy-start.3 = (bf16[2,16,144,192]{3,2,1,0:T(8,128)(2,1)}, bf16[2,16,144,192]{3,2,1,0:T(8,128)(2,1)S(1)}, u32[]{:S(2)}) copy-start(bf16[2,16,144,192]{3,2,1,0:T(8,128)(2,1)S(1)} %get-tuple-element.334) | copy-start | bytes 5308420 | tf_op jit(solution)/shard_map/while
  99.8 17.0 %copy-start.5 = (bf16[192,576]{1,0:T(8,128)(2,1)S(1)}, bf16[192,576]{1,0:T(8,128)(2,1)}, u32[]{:S(2)}) copy-start(bf16[192,576]{1,0:T(8,128)(2,1)} %get-tuple-element.329) | copy-start | bytes 663556 | tf_op jit(solution)/shard_map/while
  124.3 13.2 %copy-start.16 = (s32[2,16,144]{2,1,0:T(8,128)S(1)}, s32[2,16,144]{2,1,0:T(8,128)}, u32[]{:S(2)}) copy-start(s32[2,16,144]{2,1,0:T(8,128)} %get-tuple-element.330) | copy-start | bytes 55300 | tf_op jit(solution)/shard_map/while
  124.3 13.1 %copy-start.19 = (pred[2,16,144]{2,1,0:T(8,128)(4,1)S(1)}, pred[2,16,144]{2,1,0:T(8,128)(4,1)}, u32[]{:S(2)}) copy-start(pred[2,16,144]{2,1,0:T(8,128)(4,1)} %get-tuple-element.331) | copy-start | bytes 13828 | tf_op jit(solution)/shard_map/while
  153.8 19.3 %copy-start.7 = (f32[16,6,144]{2,1,0:T(8,128)}, f32[16,6,144]{2,1,0:T(8,128)S(1)}, u32[]{:S(2)}) copy-start(f32[16,6,144]{2,1,0:T(8,128)S(1)} %get-tuple-element.290) | copy-start | bytes 165892 | tf_op jit(solution)/shard_map/while
  153.8 9.6 %copy-start.1 = (f32[16,6,144,144]{2,3,1,0:T(8,128)S(1)}, f32[16,6,144,144]{2,3,1,0:T(8,128)}, u32[]{:S(2)}) copy-start(f32[16,6,144,144]{2,3,1,0:T(8,128)} %get-tuple-element.289) | copy-start | bytes 23887876 | tf_op jit(solution)/shard_map/while
  199.7 6.8 %copy-start.15 = (f32[192,576]{1,0:T(8,128)}, f32[192,576]{1,0:T(8,128)S(1)}, u32[]{:S(2)}) copy-start(f32[192,576]{1,0:T(8,128)S(1)} %fusion.133) | copy-start | bytes 1327108 | tf_op jit(solution)/shard_map/while
  199.7 6.8 %copy-start.4 = (bf16[2,16,144,192]{3,2,1,0:T(8,128)(2,1)S(1)}, bf16[2,16,144,192]{3,2,1,0:T(8,128)(2,1)}, u32[]{:S(2)}) copy-start(bf16[2,16,144,192]{3,2,1,0:T(8,128)(2,1)} %copy-done.3) | copy-start | bytes 5308420 | tf_op jit(solution)/shard_map/while
  199.7 6.8 %copy-start.17 = (f32[192,192]{1,0:T(8,128)S(1)}, f32[192,192]{1,0:T(8,128)}, u32[]{:S(2)}) copy-start(f32[192,192]{1,0:T(8,128)} %get-tuple-element.310) | copy-start | bytes 442372 | tf_op jit(solution)/shard_map/while
  207.2 17.1 %copy-start.18 = (f32[192,192]{1,0:T(8,128)}, f32[192,192]{1,0:T(8,128)S(1)}, u32[]{:S(2)}) copy-start(f32[192,192]{1,0:T(8,128)S(1)} %fusion.135) | copy-start | bytes 442372 | tf_op jit(solution)/shard_map/while
  224.3 34.4 %slice-start = ((s8[4718592]{0:T(1024)(128)(4,1)}), s8[524288]{0:T(1024)(128)(4,1)S(1)}, s32[]{:S(2)}) async-start(s8[4718592]{0:T(1024)(128)(4,1)} %bitcast.188), calls=%async_computation.2 | async-start | bytes 1048576 | tf_op jit(solution)/shard_map/while
  247.5 11.2 %slice-start.1 = ((s8[4718592]{0:T(1024)(128)(4,1)}), s8[4194304]{0:T(1024)(128)(4,1)S(1)}, s32[]{:S(2)}) async-start(s8[4718592]{0:T(1024)(128)(4,1)} %bitcast.188), calls=%async_computation.3 | async-start | bytes 8388608 | tf_op jit(solution)/shard_map/while
  247.5 11.2 %copy-start.6 = (bf16[192,576]{1,0:T(8,128)(2,1)S(1)}, bf16[192,576]{1,0:T(8,128)(2,1)}, u32[]{:S(2)}) copy-start(bf16[192,576]{1,0:T(8,128)(2,1)} %get-tuple-element.329) | copy-start | bytes 663556 | tf_op jit(solution)/shard_map/while
  262.7 18.3 %copy-start.3 = (bf16[2,16,144,192]{3,2,1,0:T(8,128)(2,1)}, bf16[2,16,144,192]{3,2,1,0:T(8,128)(2,1)S(1)}, u32[]{:S(2)}) copy-start(bf16[2,16,144,192]{3,2,1,0:T(8,128)(2,1)S(1)} %get-tuple-element.334) | copy-start | bytes 5308420 | tf_op jit(solution)/shard_map/while
  293.4 17.0 %copy-start.5 = (bf16[192,576]{1,0:T(8,128)(2,1)S(1)}, bf16[192,576]{1,0:T(8,128)(2,1)}, u32[]{:S(2)}) copy-start(bf16[192,576]{1,0:T(8,128)(2,1)} %get-tuple-element.329) | copy-start | bytes 663556 | tf_op jit(solution)/shard_map/while
  317.6 13.1 %copy-start.16 = (s32[2,16,144]{2,1,0:T(8,128)S(1)}, s32[2,16,144]{2,1,0:T(8,128)}, u32[]{:S(2)}) copy-start(s32[2,16,144]{2,1,0:T(8,128)} %get-tuple-element.330) | copy-start | bytes 55300 | tf_op jit(solution)/shard_map/while
  317.6 13.1 %copy-start.19 = (pred[2,16,144]{2,1,0:T(8,128)(4,1)S(1)}, pred[2,16,144]{2,1,0:T(8,128)(4,1)}, u32[]{:S(2)}) copy-start(pred[2,16,144]{2,1,0:T(8,128)(4,1)} %get-tuple-element.331) | copy-start | bytes 13828 | tf_op jit(solution)/shard_map/while
  347.1 19.3 %copy-start.7 = (f32[16,6,144]{2,1,0:T(8,128)}, f32[16,6,144]{2,1,0:T(8,128)S(1)}, u32[]{:S(2)}) copy-start(f32[16,6,144]{2,1,0:T(8,128)S(1)} %get-tuple-element.290) | copy-start | bytes 165892 | tf_op jit(solution)/shard_map/while
  347.1 9.6 %copy-start.1 = (f32[16,6,144,144]{2,3,1,0:T(8,128)S(1)}, f32[16,6,144,144]{2,3,1,0:T(8,128)}, u32[]{:S(2)}) copy-start(f32[16,6,144,144]{2,3,1,0:T(8,128)} %get-tuple-element.289) | copy-start | bytes 23887876 | tf_op jit(solution)/shard_map/while
  393.0 6.8 %copy-start.15 = (f32[192,576]{1,0:T(8,128)}, f32[192,576]{1,0:T(8,128)S(1)}, u32[]{:S(2)}) copy-start(f32[192,576]{1,0:T(8,128)S(1)} %fusion.133) | copy-start | bytes 1327108 | tf_op jit(solution)/shard_map/while
  400.5 17.1 %copy-start.18 = (f32[192,192]{1,0:T(8,128)}, f32[192,192]{1,0:T(8,128)S(1)}, u32[]{:S(2)}) copy-start(f32[192,192]{1,0:T(8,128)S(1)} %fusion.135) | copy-start | bytes 442372 | tf_op jit(solution)/shard_map/while
  417.6 36.5 %slice-start = ((s8[4718592]{0:T(1024)(128)(4,1)}), s8[524288]{0:T(1024)(128)(4,1)S(1)}, s32[]{:S(2)}) async-start(s8[4718592]{0:T(1024)(128)(4,1)} %bitcast.188), calls=%async_computation.2 | async-start | bytes 1048576 | tf_op jit(solution)/shard_map/while
  440.8 13.3 %slice-start.1 = ((s8[4718592]{0:T(1024)(128)(4,1)}), s8[4194304]{0:T(1024)(128)(4,1)S(1)}, s32[]{:S(2)}) async-start(s8[4718592]{0:T(1024)(128)(4,1)} %bitcast.188), calls=%async_computation.3 | async-start | bytes 8388608 | tf_op jit(solution)/shard_map/while
  440.8 13.3 %copy-start.6 = (bf16[192,576]{1,0:T(8,128)(2,1)S(1)}, bf16[192,576]{1,0:T(8,128)(2,1)}, u32[]{:S(2)}) copy-start(bf16[192,576]{1,0:T(8,128)(2,1)} %get-tuple-element.329) | copy-start | bytes 663556 | tf_op jit(solution)/shard_map/while
  469.2 143.3 %all-reduce.5.cloned.1.call-start = ((), (), s32[]{:S(2)}) async-start(), calls=%async_computation | async-start | bytes 11304960 | tf_op jit(solution)/shard_map/psum | solution.py:190
  519.7 8.3 %collective-permute-start.4 = (bf16[8,3,24,192]{3,0,2,1:T(8,128)(2,1)S(1)}, bf16[8,3,24,192]{3,0,2,1:T(8,128)(2,1)S(1)}, u32[]{:S(2)}, u32[]{:S(2)}) collective-permute-start(bf16[8,3,24,192]{3,0,2,1:T(8,128)(2,1)S(1)} %slice.99), channel_id=1, source_target_pairs={{0,1},{1,2},{2,3},{4,5},{5,6},{6,7},{8,9},{9,10},{10,11},{12,13},{... | collective-permute-start | bytes 663560 | tf_op jit(solution)/shard_map/ppermute | solution.py:22
  528.1 19.4 %collective-permute-start.5 = (bf16[8,24,6,192]{3,0,2,1:T(8,128)(2,1)S(1)}, bf16[8,24,6,192]{3,0,2,1:T(8,128)(2,1)S(1)}, u32[]{:S(2)}, u32[]{:S(2)}) collective-permute-start(bf16[8,24,6,192]{3,0,2,1:T(8,128)(2,1)S(1)} %pad_maximum_fusion.7), channel_id=1, source_target_pairs={{28,0},{0,4},{4,8},{8,12},{12,16},{16,20},{20,24},{24,28},{29,1},{... | collective-permute-start | bytes 1327112 | tf_op jit(solution)/shard_map/ppermute | solution.py:16
  (22 other events, 71.5 us)
Sparse Core Ops, SparseCore 0:
  469.3 36.3 all-reduce.6
  510.0 102.4 all-reduce.4
where the time goes:
time: 635 us; the launch traced here: 629 us
  local copies, waits for them, and re-layouts  244 us (38%)
  matrix products  161 us (25%)
  waiting for transfers between devices  110 us (17%)
  other arithmetic  79.9 us (13%)
  between operations  14.5 us (2%)
  starting transfers between devices  11.1 us (2%)
  loops' own time  9.27 us (1%)
    dot_general x4, local copies, waits for them, and re-layouts, window_backward(): jnp.dot(block_types.astype(jnp.bfloat16), bias_rows, preferred_element_ty...  64.3 us
    psum x1, waiting for transfers between devices, local(): lax.psum(totals[2].astype(jnp.bfloat16), 'lon').astype(jnp.float32)  61.7 us
    reshape x2, local copies, waits for them, and re-layouts, window_backward(): score_grad.reshape(windows, -1)  46.5 us
    mul x2, local copies, waits for them, and re-layouts, window_backward(): score_grad = attn_probs * (prob_grad - row_delta)  34.2 us
    sub x2, other arithmetic, window_backward(): exp_terms = jnp.where(allowed, jnp.exp(scores - peak_score), 0.0)  30.7 us
    dot_general x2, matrix products, window_backward(): jnp.einsum('bqhd,bkhd->bhqk', queries, key_rows, preferred_element_type=f32)  26.3 us
    dot_general x2, matrix products, window_backward(): jnp.dot(block_types.astype(jnp.bfloat16), bias_rows, preferred_element_ty...  24.7 us
    dot_general x2, matrix products, window_backward(): jnp.dot(block_types.T, score_grad.reshape(windows, -1), precision=high, p...  24.4 us
  transfers between devices with their start and end apart: 8, of which 5 were waited for; matrix products, arithmetic and copies ran while one was open for 10% of the time, Pallas kernels for 0%

commit v1 on v0

v1 whole, which is shorter than its diff:
```python
import functools
import math

import jax
import jax.numpy as jnp
from jax import lax
from jax.experimental import pallas as pl
from jax.experimental.pallas import tpu as pltpu
from jax.sharding import PartitionSpec as P

HEADS = 6
WIN_Z = 2
WIN_LAT = 6
WIN_LON = 12
WTOK = 144
LANES = 128
TAIL = WTOK - LANES
HALO = 8
CHUNKS = 2
LOG2E = math.log2(math.e)
F32 = jnp.float32
BF16 = jnp.bfloat16


def ring_permute(block, axis, distance):
    size = lax.axis_size(axis)
    return lax.ppermute(block, axis, [((i - distance) % size, i) for i in range(size)])


def line_permute(block, axis, distance):
    size = lax.axis_size(axis)
    route = [(i - distance, i) for i in range(size) if 0 <= i - distance < size]
    return lax.ppermute(block, axis, route)


def mm(a, b, ca=1, cb=0):
    return lax.dot_general(a, b, (((ca,), (cb,)), ((), ())), preferred_element_type=F32)


def kernel(
    first_row,
    lat_windows,
    level_windows,
    lon_windows,
    last_ref,
    perm_ref,
    xa_ref,
    xb_ref,
    ca_ref,
    cb_ref,
    wqkv_ref,
    wproj_ref,
    bias_ref,
    gframe_ref,
    gqkv_ref,
    gproj_ref,
    gbias_ref,
    qm_s,
    mm_s,
    p_s,
    ds_s,
):
    step = pl.program_id(0)
    a = lax.rem(step, level_windows)
    b = step // level_windows + first_row
    channels = wqkv_ref.shape[0]
    head_dim = channels // HEADS
    scale = head_dim ** -0.5
    half = WIN_LAT * xa_ref.shape[2]

    @pl.when(step == 0)
    def _():
        gqkv_ref[...] = jnp.zeros_like(gqkv_ref)
        gproj_ref[...] = jnp.zeros_like(gproj_ref)

    perm = perm_ref[...]
    x_raw = jnp.concatenate(
        [xa_ref[...].reshape(half, channels), xb_ref[...].reshape(half, channels)], axis=0
    )
    c_raw = jnp.concatenate(
        [ca_ref[...].reshape(half, channels), cb_ref[...].reshape(half, channels)], axis=0
    )
    x = mm(perm, x_raw).astype(BF16)
    c = mm(perm, c_raw).astype(BF16)
    proj = mm(x, wqkv_ref[...]).astype(BF16)
    mgrad = mm(c, wproj_ref[...], 1, 1).astype(BF16)

    wrap_here = a == level_windows - 1
    dead_here = (b == lat_windows - 1) & (last_ref[0] == 1)
    per_level = WTOK // WIN_Z

    def classes(shape, dim):
        token = lax.broadcasted_iota(jnp.int32, shape, dim)
        upper = token >= per_level
        inner = jnp.where(upper, token - per_level, token)
        wrapped = jnp.where(upper & wrap_here, 2, 0)
        dead = jnp.where((inner >= per_level // 2) & dead_here, 1, 0)
        return wrapped + dead

    same = classes((WTOK, WTOK), 0) == classes((WTOK, WTOK), 1)
    mask_add = jnp.where(same, 0.0, -1e30)
    lane_head = lax.broadcasted_iota(jnp.int32, (1, channels), 1) // head_dim
    zero = jnp.zeros((), BF16)

    parts = []
    for w in range(lon_windows):
        rows = slice(w * WTOK, (w + 1) * WTOK)
        parts.append(
            (
                proj[rows, :channels],
                proj[rows, channels : 2 * channels],
                proj[rows, 2 * channels :],
                mgrad[rows],
            )
        )
    mixed = [jnp.zeros((WTOK, channels), F32) for _ in range(lon_windows)]
    dq = [jnp.zeros((WTOK, channels), F32) for _ in range(lon_windows)]
    for h in range(HEADS):
        hot = (lane_head == h).astype(BF16)
        hrows = slice(h * WTOK, (h + 1) * WTOK)
        shift = bias_ref[0, hrows, :].astype(F32) * LOG2E + mask_add
        gb = None
        for w in range(lon_windows):
            q, k, v, m = parts[w]
            qm = q * hot
            mg = m * hot
            qm_s[w, hrows, :] = qm
            mm_s[w, hrows, :] = mg
            s = mm(qm, k, 1, 1) * (scale * LOG2E) + shift
            dp = mm(mg, v, 1, 1)
            e = jnp.exp2(s - jnp.max(s, axis=1, keepdims=True))
            p = e * (1.0 / jnp.sum(e, axis=1, keepdims=True))
            delta = jnp.sum(p * dp, axis=1, keepdims=True)
            ds = p * (dp - delta)
            pb = p.astype(BF16)
            dsb = ds.astype(BF16)
            p_s[w, hrows, :] = pb
            ds_s[w, hrows, :] = dsb
            gb = ds if gb is None else gb + ds
            mixed[w] = mixed[w] + mm(pb, v * hot)
            dq[w] = dq[w] + mm(dsb, k * hot)
        gb = gb.astype(BF16)
        gbias_ref[0, hrows, :] = gb[:, :LANES]
        gbias_ref[0, HEADS * WTOK :, h * TAIL : (h + 1) * TAIL] = gb[:, LANES:]
    cols = []
    for w in range(lon_windows):
        dk = mm(ds_s[w], qm_s[w], 0, 0) * scale
        dv = mm(p_s[w], mm_s[w], 0, 0)
        cols.append(
            jnp.concatenate(
                [(dq[w] * scale).astype(BF16), dk.astype(BF16), dv.astype(BF16)], axis=1
            )
        )
    cols = jnp.concatenate(cols, axis=0)
    mixed_b = jnp.concatenate([t.astype(BF16) for t in mixed], axis=0)
    gproj_ref[...] += mm(mixed_b, c, 0, 0)
    gqkv_ref[...] += mm(x, cols, 0, 0)
    gin = mm(cols, wqkv_ref[...], 1, 1).astype(BF16)
    gout = mm(perm, gin, 0, 0).astype(BF16)
    gframe_ref[...] = gout.reshape(gframe_ref.shape)


def window_call(chunk, last, perm, frame_in, frame_cot, weight_qkv, weight_proj, bias):
    levels, height, wide, channels = frame_in.shape
    level_windows = levels // WIN_Z
    lat_windows = height // WIN_LAT
    lon_windows = perm.shape[0] // WTOK
    rows_here = lat_windows // CHUNKS
    first = chunk * rows_here
    kinds = rows_here * level_windows

    def at(step, up):
        z = lax.rem(WIN_Z * lax.rem(step, level_windows) + up, levels)
        return z, step // level_windows + first, 0, 0

    tok = (1, WIN_LAT, wide, channels)
    low = pl.BlockSpec(tok, lambda i: at(i, 1))
    high = pl.BlockSpec(tok, lambda i: at(i, 2))
    whole = lambda arr: pl.BlockSpec(arr.shape, lambda i: (0,) * arr.ndim)
    const = lambda shape: pl.BlockSpec(shape, lambda i: (0,) * len(shape))
    stack = HEADS * WTOK
    packed = stack + WTOK
    return pl.pallas_call(
        functools.partial(kernel, first, lat_windows, level_windows, lon_windows),
        grid=(kinds,),
        in_specs=[
            pl.BlockSpec(memory_space=pltpu.SMEM),
            whole(perm),
            low,
            high,
            low,
            high,
            whole(weight_qkv),
            whole(weight_proj),
            pl.BlockSpec((1, stack, WTOK), lambda i: (i + first * level_windows, 0, 0)),
        ],
        out_specs=[
            pl.BlockSpec(
                (WIN_Z, WIN_LAT, wide, channels),
                lambda i: (lax.rem(i, level_windows), i // level_windows, 0, 0),
            ),
            const((channels, 3 * channels)),
            const((channels, channels)),
            pl.BlockSpec((1, packed, LANES), lambda i: (i, 0, 0)),
        ],
        out_shape=[
            jax.ShapeDtypeStruct((levels, rows_here * WIN_LAT, wide, channels), BF16),
            jax.ShapeDtypeStruct((channels, 3 * channels), F32),
            jax.ShapeDtypeStruct((channels, channels), F32),
            jax.ShapeDtypeStruct((kinds, packed, LANES), BF16),
        ],
        scratch_shapes=[
            pltpu.VMEM((lon_windows, stack, channels), BF16),
            pltpu.VMEM((lon_windows, stack, channels), BF16),
            pltpu.VMEM((lon_windows, stack, WTOK), BF16),
            pltpu.VMEM((lon_windows, stack, WTOK), BF16),
        ],
        compiler_params=pltpu.CompilerParams(
            dimension_semantics=("arbitrary",), vmem_limit_bytes=48 * 2**20
        ),
        cost_estimate=pl.CostEstimate(
            flops=kinds * 1_500_000_000, bytes_accessed=kinds * 2_000_000, transcendentals=0
        ),
    )(
        last, perm, frame_in, frame_in, frame_cot, frame_cot, weight_qkv, weight_proj, bias
    )


def local(normed, cotangent, weight_qkv, weight_proj, bias_table):
    levels, height, breadth, channels = normed.shape
    lat_shift = WIN_LAT // 2
    lon_shift = WIN_LON // 2
    level_windows = levels // WIN_Z
    lat_windows = height // WIN_LAT
    lon_windows = breadth // WIN_LON
    types_local = level_windows * lat_windows
    wide = breadth + HALO
    across = ring_permute((normed[:, :, :HALO], cotangent[:, :, :HALO]), "lon", -1)
    wide_in = jnp.concatenate([normed, across[0]], axis=2)
    wide_cot = jnp.concatenate([cotangent, across[1]], axis=2)
    upward = line_permute((wide_in[:, :lat_shift], wide_cot[:, :lat_shift]), "lat", -1)
    frame_in = jnp.concatenate([wide_in[:, lat_shift:], upward[0]], axis=1)
    frame_cot = jnp.concatenate([wide_cot[:, lat_shift:], upward[1]], axis=1)
    last = (lax.axis_index("lat") == lax.axis_size("lat") - 1).astype(jnp.int32).reshape(1)
    bias = bias_table.reshape(types_local, HEADS * WTOK, WTOK)

    rows = jnp.arange(lon_windows * WTOK, dtype=jnp.int32)
    token = rows % WTOK
    per_level = WIN_LAT * WIN_LON
    source = (
        token // per_level * (WIN_LAT * wide)
        + token % per_level // WIN_LON * wide
        + rows // WTOK * WIN_LON
        + token % WIN_LON
        + lon_shift
    )
    columns = jnp.arange(WIN_Z * WIN_LAT * wide, dtype=jnp.int32)
    perm = (source[:, None] == columns[None, :]).astype(BF16)

    frames, qkv, proj, biases = [], 0.0, 0.0, []
    for chunk in range(CHUNKS):
        gframe, gqkv, gproj, gbias = window_call(
            chunk, last, perm, frame_in, frame_cot, weight_qkv, weight_proj, bias
        )
        frames.append(gframe)
        qkv = qkv + gqkv
        proj = proj + gproj
        biases.append(lax.psum(gbias, "lon"))

    gwide = jnp.roll(jnp.concatenate(frames, axis=1), WIN_Z // 2, axis=0)
    side = ring_permute(gwide[:, :, breadth:], "lon", 1)
    seam = jnp.concatenate(
        [gwide[:, :, :HALO] + side, gwide[:, :, HALO:breadth]], axis=2
    )
    down = line_permute(seam[:, height - lat_shift :], "lat", 1)
    input_grad = jnp.concatenate([down, seam[:, : height - lat_shift]], axis=1)
    qkv_grad, proj_grad = lax.psum((qkv.astype(BF16), proj.astype(BF16)), ("lat", "lon"))

    stack = HEADS * WTOK
    outs = []
    for packed in biases:
        kinds = packed.shape[0]
        head = packed[:, :stack].reshape(kinds, HEADS, WTOK, LANES)
        tail = packed[:, stack:, : HEADS * TAIL].reshape(kinds, WTOK, HEADS, TAIL)
        both = jnp.concatenate([head, tail.transpose(0, 2, 1, 3)], axis=3)
        outs.append(both.astype(F32).reshape(kinds, HEADS, WTOK * WTOK))
    bias_grad = jnp.concatenate(outs, axis=0)
    return input_grad, qkv_grad.astype(F32), proj_grad.astype(F32), bias_grad


def solution(mesh):
    in_specs = (
        P(None, "lat", "lon", None),
        P(None, "lat", "lon", None),
        P(),
        P(),
        P("lat", None, None),
    )
    out_specs = (P(None, "lat", "lon", None), P(), P(), P("lat", None, None))
    return jax.shard_map(local, mesh=mesh, in_specs=in_specs, out_specs=out_specs, check_vma=False)
```

time: 635 us -> 423 us (0.67)
  local copies, waits for them, and re-layouts: 244 us -> 55.2 us
  matrix products: 161 us -> 0 us
  waiting for transfers between devices: 110 us -> 217 us
  Pallas kernels: 0 us -> 101 us
  other arithmetic: 79.9 us -> 23.6 us
  loops' own time: 9.27 us -> 0 us
    dot_general x26 -> x0, matrix products: 161 us -> none  [the longest x2 26.3 us: window_backward(): jnp.einsum('bqhd,bkhd->bhqk', queries, key_rows, preferred_element_type=f32)]
    psum x2, waiting for transfers between devices: 83.6 us -> 190 us  [the longest x1 111 us: local(): lax.psum((qkv.astype(BF16), proj.astype(BF16)), ('lat', 'lon'))]
    pallas_call x0 -> x2, Pallas kernels: none -> 101 us  [window_call(): pl.pallas_call(functools.partial(kernel, first, lat_windows, level_window...]
    dot_general x4 -> x0, local copies, waits for them, and re-layouts: 64.3 us -> none  [window_backward(): jnp.dot(block_types.astype(jnp.bfloat16), bias_rows, preferred_element_ty...]
    reshape x7 -> x1, local copies, waits for them, and re-layouts: 70.1 us -> 13.8 us  [local(): bias = bias_table.reshape(types_local, HEADS * WTOK, WTOK)]
    mul x2 -> x0, local copies, waits for them, and re-layouts: 34.2 us -> none  [window_backward(): score_grad = attn_probs * (prob_grad - row_delta)]
    sub x2 -> x0, other arithmetic: 30.7 us -> none  [window_backward(): exp_terms = jnp.where(allowed, jnp.exp(scores - peak_score), 0.0)]
    mul x3 -> x0, other arithmetic: 20.2 us -> none  [the longest x2 20.2 us: window_backward(): score_grad = attn_probs * (prob_grad - row_delta)]
  transfers between devices with their start and end apart: 8 -> 8, of which waited for: 5 -> 5; matrix products, arithmetic and copies ran while one was open for 10% -> 8% of each run, Pallas kernels for 0% -> 0%
where the time goes in v1:
time: 423 us; the launch traced here: 422 us
  waiting for transfers between devices  217 us (51%)
  Pallas kernels  101 us (24%)
  local copies, waits for them, and re-layouts  55.2 us (13%)
  other arithmetic  23.6 us (6%)
  between operations  14.3 us (3%)
  starting transfers between devices  11.8 us (3%)
    psum x1, waiting for transfers between devices, local(): lax.psum((qkv.astype(BF16), proj.astype(BF16)), ('lat', 'lon'))  111 us
    pallas_call x2, Pallas kernels, window_call(): pl.pallas_call(functools.partial(kernel, first, lat_windows, level_window...  101 us
    psum x1, waiting for transfers between devices, local(): biases.append(lax.psum(gbias, 'lon'))  79.4 us
    ppermute x3, waiting for transfers between devices, ring_permute(): lax.ppermute(block, axis, [((i - distance) % size, i) for i in range(size)])  25.6 us
    convert_element_type x4, local copies, waits for them, and re-layouts, local(): outs.append(both.astype(F32).reshape(kinds, HEADS, WTOK * WTOK))  17.7 us
    reshape x1, local copies, waits for them, and re-layouts, local(): bias = bias_table.reshape(types_local, HEADS * WTOK, WTOK)  13.8 us
  transfers between devices with their start and end apart: 8, of which 5 were waited for; matrix products, arithmetic and copies ran while one was open for 8% of the time, Pallas kernels for 0%

profile of v1, /device:TPU:0, one launch (start us, length us, event | category | flops | bytes accessed | tf_op | source)
XLA Modules:
  0.0 422.2 jit_solution(6673011070227859831)
XLA Ops:
  7.2 1.3 slice.53
  8.6 3.4 collective-permute-start
  12.0 1.2 slice.56
  14.6 6.9 %collective-permute-done = bf16[8,24,8,192]{3,2,1,0:T(8,128)(2,1)S(1)} collective-permute-done((bf16[8,24,8,192]{3,2,1,0:T(8,128)(2,1)S(1)}, bf16[8,24,8,192]{3,2,1,0:T(8,128)(2,1)S(1)}, u32[]{:S(2)}, u32[]{:S(2)}) %collective-permute-start) | collective-permute-done | bytes 589856 | tf_op jit(solution)/shard_map/ppermute | solution.py:27
  22.5 1.3 collective-permute-start.1
  23.7 6.2 %collective-permute-done.2 = bf16[8,24,8,192]{3,2,1,0:T(8,128)(2,1)S(1)} collective-permute-done((bf16[8,24,8,192]{3,2,1,0:T(8,128)(2,1)S(1)}, bf16[8,24,8,192]{3,2,1,0:T(8,128)(2,1)S(1)}, u32[]{:S(2)}, u32[]{:S(2)}) %collective-permute-start.2) | collective-permute-done | bytes 589856 | tf_op jit(solution)/shard_map/ppermute | solution.py:27
  30.8 1.3 collective-permute-start.3
  32.2 5.7 %copy.14 = bf16[16,6,20736]{2,1,0:T(8,128)(2,1)} copy(bf16[16,6,20736]{2,0,1:T(8,128)(2,1)} %param.9) | data formatting | bytes 7962624 | tf_op args[4]
  37.9 13.8 %reshape.88.bias_ref = bf16[16,864,144]{2,1,0:T(8,128)(2,1)} reshape(bf16[16,6,20736]{2,1,0:T(8,128)(2,1)} %copy.14) | data formatting | bytes 7962624 | tf_op jit(solution)/shard_map/reshape | solution.py:245
  51.8 2.0 slice.70
  54.1 3.2 pad_maximum_fusion.2.xa_ref.xb_ref
  57.2 3.2 pad_maximum_fusion.3.ca_ref.cb_ref
  60.5 50.4 %shard_map.85 = (bf16[8,12,32,192]{3,2,1,0:T(8,128)(2,1)S(1)}, f32[192,576]{1,0:T(8,128)S(1)}, f32[192,192]{1,0:T(8,128)S(1)}, bf16[8,1008,128]{2,1,0:T(8,128)(2,1)}) custom-call(s32[1]{0:T(128)} %bitcast.last_ref, bf16[288,384]{1,0:T(8,128)(2,1)S(1)} %fusion.4.perm_ref, bf16[8,24,32,192]{3,2,1,0:T(8,128)(2,1)} %pad_maximum_fusion.2.xa_ref.xb_ref, ...), custom_call_target="tpu_custom_call" | custom-call | flops 12000000000 | bytes 16000000 | tf_op jit(solution)/shard_map/pallas_call | solution.py:183
  110.9 50.4 %shard_map.84 = (bf16[8,12,32,192]{3,2,1,0:T(8,128)(2,1)S(1)}, f32[192,576]{1,0:T(8,128)S(1)}, f32[192,192]{1,0:T(8,128)S(1)}, bf16[8,1008,128]{2,1,0:T(8,128)(2,1)}) custom-call(s32[1]{0:T(128)} %bitcast.last_ref, bf16[288,384]{1,0:T(8,128)(2,1)S(1)} %fusion.4.perm_ref, bf16[8,24,32,192]{3,2,1,0:T(8,128)(2,1)} %pad_maximum_fusion.2.xa_ref.xb_ref, ...), custom_call_target="tpu_custom_call" | custom-call | flops 12000000000 | bytes 16000000 | tf_op jit(solution)/shard_map/pallas_call | solution.py:183
  164.7 12.5 %collective-permute-done.4 = bf16[8,24,8,192]{3,2,1,0:T(8,128)(2,1)S(1)} collective-permute-done((bf16[8,24,8,192]{3,2,1,0:T(8,128)(2,1)S(1)}, bf16[8,24,8,192]{3,2,1,0:T(8,128)(2,1)S(1)}, u32[]{:S(2)}, u32[]{:S(2)}) %collective-permute-start.4) | collective-permute-done | bytes 589856 | tf_op jit(solution)/shard_map/ppermute | solution.py:27
  178.1 4.4 %collective-permute-start.5 = (bf16[8,3,24,192]{3,2,1,0:T(8,128)(2,1)S(1)}, bf16[8,3,24,192]{3,2,1,0:T(8,128)(2,1)S(1)}, u32[]{:S(2)}, u32[]{:S(2)}) collective-permute-start(bf16[8,3,24,192]{3,2,1,0:T(8,128)(2,1)S(1)} %slice.76), channel_id=1, source_target_pairs={{0,1},{1,2},{2,3},{4,5},{5,6},{6,7},{8,9},{9,10},{10,11},{12,13},{... | collective-permute-start | bytes 663560 | tf_op jit(solution)/shard_map/ppermute | solution.py:33
  182.5 111.1 %all-reduce.5.cloned.1.call-done = (bf16[192,576]{1,0:T(8,128)(2,1)}, bf16[192,192]{1,0:T(8,128)(2,1)}) async-done(((bf16[192,576]{1,0:T(8,128)(2,1)}, bf16[192,192]{1,0:T(8,128)(2,1)}), (bf16[192,576]{1,0:T(8,128)(2,1)}, bf16[192,192]{1,0:T(8,128)(2,1)})) %all-reduce.5.cloned.1.call-update) | async-done | bytes 294928 | tf_op jit(solution)/shard_map/psum | solution.py:277
  293.6 1.6 convert_element_type.32
  295.2 1.8 convert_element_type.30
  297.1 1.8 pad_maximum_fusion.4
  298.9 79.4 %all-reduce.7.cloned.1.call-done = (bf16[8,1008,128]{2,1,0:T(8,128)(2,1)}, bf16[8,1008,128]{2,1,0:T(8,128)(2,1)}) async-done(((bf16[8,1008,128]{2,1,0:T(8,128)(2,1)}, bf16[8,1008,128]{2,1,0:T(8,128)(2,1)}), (bf16[8,1008,128]{2,1,0:T(8,128)(2,1)}, bf16[8,1008,128]{2,1,0:T(8,128)(2,1)})) %all-reduce.7.cloned.1.call-update) | async-done | bytes 4128784 | tf_op jit(solution)/shard_map/psum | solution.py:268
  379.4 2.8 slice.80
  382.2 1.4 slice.78
  384.8 1.6 copy.16
  386.4 2.9 pad_maximum_fusion
  389.2 6.1 %reshape.95 = bf16[8,6,20736]{2,1,0:T(8,128)(2,1)} reshape(bf16[8,6,144,144]{3,2,1,0:T(8,128)(2,1)S(1)} %pad_maximum_fusion) | data formatting | bytes 3981312 | tf_op jit(solution)/shard_map/convert_element_type | solution.py:286
  395.3 3.4 copy.21
  398.7 1.6 copy.19
  400.3 2.9 pad_maximum_fusion.1
  403.2 6.1 %reshape.96 = bf16[8,6,20736]{2,1,0:T(8,128)(2,1)} reshape(bf16[8,6,144,144]{3,2,1,0:T(8,128)(2,1)S(1)} %pad_maximum_fusion.1) | data formatting | bytes 3981312 | tf_op jit(solution)/shard_map/convert_element_type | solution.py:286
  409.2 2.2 copy.22
  411.6 3.8 maximum_convert_fusion
  (49 shorter events, 10.4 us)
Async XLA Ops:
  7.2 6.8 %copy-start.4 = (bf16[8,24,24,192]{3,2,1,0:T(8,128)(2,1)S(1)}, bf16[8,24,24,192]{3,2,1,0:T(8,128)(2,1)}, u32[]{:S(2)}) copy-start(bf16[8,24,24,192]{3,2,1,0:T(8,128)(2,1)} %param.5) | copy-start | bytes 5308420
  7.2 286.4 %all-reduce.5.cloned.1.call-start = ((), (), s32[]{:S(2)}) async-start(), calls=%async_computation | async-start | bytes 688128 | tf_op jit(solution)/shard_map/psum | solution.py:277
  8.6 5.7 %copy-start.5 = (bf16[8,24,24,192]{3,2,1,0:T(8,128)(2,1)S(1)}, bf16[8,24,24,192]{3,2,1,0:T(8,128)(2,1)}, u32[]{:S(2)}) copy-start(bf16[8,24,24,192]{3,2,1,0:T(8,128)(2,1)} %param.6) | copy-start | bytes 5308420
  8.6 12.9 %collective-permute-start = (bf16[8,24,8,192]{3,2,1,0:T(8,128)(2,1)S(1)}, bf16[8,24,8,192]{3,2,1,0:T(8,128)(2,1)S(1)}, u32[]{:S(2)}, u32[]{:S(2)}) collective-permute-start(bf16[8,24,8,192]{3,2,1,0:T(8,128)(2,1)S(1)} %slice.53), channel_id=1, source_target_pairs={{4,0},{8,4},{12,8},{16,12},{20,16},{24,20},{28,24},{0,28},{5,1},{9... | collective-permute-start | bytes 1769480 | tf_op jit(solution)/shard_map/ppermute | solution.py:27
  13.2 16.7 %collective-permute-start.2 = (bf16[8,24,8,192]{3,2,1,0:T(8,128)(2,1)S(1)}, bf16[8,24,8,192]{3,2,1,0:T(8,128)(2,1)S(1)}, u32[]{:S(2)}, u32[]{:S(2)}) collective-permute-start(bf16[8,24,8,192]{3,2,1,0:T(8,128)(2,1)S(1)} %slice.56), channel_id=1, source_target_pairs={{4,0},{8,4},{12,8},{16,12},{20,16},{24,20},{28,24},{0,28},{5,1},{9... | collective-permute-start | bytes 1769480 | tf_op jit(solution)/shard_map/ppermute | solution.py:27
  21.6 9.2 %copy-start.2 = (bf16[8,24,32,192]{3,2,1,0:T(8,128)(2,1)}, bf16[8,24,32,192]{3,2,1,0:T(8,128)(2,1)S(1)}, u32[]{:S(2)}) copy-start(bf16[8,24,32,192]{3,2,1,0:T(8,128)(2,1)S(1)} %constant_dynamic-update-slice_fusion) | copy-start | bytes 7077892
  22.5 31.6 %collective-permute-start.1 = (bf16[8,3,32,192]{3,2,1,0:T(8,128)(2,1)}, bf16[8,3,32,192]{3,2,1,0:T(8,128)(2,1)}, u32[]{:S(2)}, u32[]{:S(2)}) collective-permute-start(bf16[8,3,32,192]{3,2,1,0:T(8,128)(2,1)} %slice.71), channel_id=1, source_target_pairs={{1,0},{2,1},{3,2},{5,4},{6,5},{7,6},{9,8},{10,9},{11,10},{13,12},{... | collective-permute-start | bytes 884744 | tf_op jit(solution)/shard_map/ppermute | solution.py:33
  30.8 26.4 %collective-permute-start.3 = (bf16[8,3,32,192]{3,2,1,0:T(8,128)(2,1)}, bf16[8,3,32,192]{3,2,1,0:T(8,128)(2,1)}, u32[]{:S(2)}, u32[]{:S(2)}) collective-permute-start(bf16[8,3,32,192]{3,2,1,0:T(8,128)(2,1)} %slice.73), channel_id=1, source_target_pairs={{1,0},{2,1},{3,2},{5,4},{6,5},{7,6},{9,8},{10,9},{11,10},{13,12},{... | collective-permute-start | bytes 884744 | tf_op jit(solution)/shard_map/ppermute | solution.py:33
  57.2 3.3 copy-start
  57.2 3.3 copy-start.1
  162.7 215.5 %all-reduce.7.cloned.1.call-start = ((), (), s32[]{:S(2)}) async-start(), calls=%async_computation.1 | async-start | bytes 8257536 | tf_op jit(solution)/shard_map/psum | solution.py:268
  164.4 12.8 %collective-permute-start.4 = (bf16[8,24,8,192]{3,2,1,0:T(8,128)(2,1)S(1)}, bf16[8,24,8,192]{3,2,1,0:T(8,128)(2,1)S(1)}, u32[]{:S(2)}, u32[]{:S(2)}) collective-permute-start(bf16[8,24,8,192]{3,2,1,0:T(8,128)(2,1)S(1)} %pad_maximum_fusion.5), channel_id=1, source_target_pairs={{28,0},{0,4},{4,8},{8,12},{12,16},{16,20},{20,24},{24,28},{29,1},{... | collective-permute-start | bytes 1769480 | tf_op jit(solution)/shard_map/ppermute | solution.py:27
  178.1 119.0 %collective-permute-start.5 = (bf16[8,3,24,192]{3,2,1,0:T(8,128)(2,1)S(1)}, bf16[8,3,24,192]{3,2,1,0:T(8,128)(2,1)S(1)}, u32[]{:S(2)}, u32[]{:S(2)}) collective-permute-start(bf16[8,3,24,192]{3,2,1,0:T(8,128)(2,1)S(1)} %slice.76), channel_id=1, source_target_pairs={{0,1},{1,2},{2,3},{4,5},{5,6},{6,7},{8,9},{9,10},{10,11},{12,13},{... | collective-permute-start | bytes 663560 | tf_op jit(solution)/shard_map/ppermute | solution.py:33
  378.2 4.0 copy-start.6
  395.3 3.4 copy-start.7
  409.2 2.4 copy-start.3
Sparse Core Ops, SparseCore 0:
  162.9 130.7 all-reduce.4
  297.0 81.2 all-reduce.6

commit v2 on v1

--- a/solution.py
+++ b/solution.py
@@ -16,7 +16,7 @@
 LANES = 128
 TAIL = WTOK - LANES
 HALO = 8
-CHUNKS = 2
+CHUNKS = 1
 LOG2E = math.log2(math.e)
 F32 = jnp.float32
 BF16 = jnp.bfloat16
@@ -160,6 +160,181 @@
     gframe_ref[...] = gout.reshape(gframe_ref.shape)
 
 
+def reduce_kernel(
+    n, lats, gb_ref, wg_ref, out_ref, wout_ref, pair_s, send_s, recv_s, w1_s, w2_s,
+    pair_sem, cross_sem, back_sem, fwd_sem, w1_sem, w2_sem, w3_sem,
+):
+    chips = n // 2
+    me = lax.axis_index("lon")
+    lat = lax.axis_index("lat")
+    core = lax.rem(me, 2)
+    chip = me // 2
+    other = 1 - core
+    partner = chip * 2 + other
+    types = gb_ref.shape[0]
+    share = types // n
+
+    def piece(which, where):
+        return pl.ds((which * chips + where) * share, share)
+
+    def copy(src, dst, sems, out_at, in_at, device):
+        return pltpu.make_async_remote_copy(
+            src_ref=src,
+            dst_ref=dst,
+            send_sem=sems.at[0, out_at],
+            recv_sem=sems.at[1, in_at],
+            device_id=device,
+            device_id_type=pl.DeviceIdType.MESH,
+        )
+
+    barrier = pltpu.get_barrier_semaphore()
+    for o in range(1, n):
+        pl.semaphore_signal(
+            barrier, inc=1, device_id={"lon": lax.rem(me + o, n)},
+            device_id_type=pl.DeviceIdType.MESH,
+        )
+    for o in range(1, lats):
+        pl.semaphore_signal(
+            barrier, inc=1, device_id={"lat": lax.rem(lat + o, lats)},
+            device_id_type=pl.DeviceIdType.MESH,
+        )
+    pl.semaphore_wait(barrier, n + lats - 2)
+
+    order = [(o, lax.rem(chip + o, chips)) for o in list(range(1, chips)) + [0]]
+    sends = []
+    first = []
+    for o in range(1, n):
+        p = lax.rem(me + o, n)
+        cp = copy(wg_ref.at[p], w1_s.at[me], w1_sem, p, me, {"lon": p})
+        cp.start()
+        sends.append(cp)
+    for o, j in order:
+        cp = copy(gb_ref.at[piece(other, j)], pair_s.at[o], pair_sem, o, o, {"lon": partner})
+        cp.start()
+        first.append(cp)
+    sends += first
+
+    w1_s[pl.ds(me, 1)] = wg_ref[pl.ds(me, 1)]
+    for o in range(1, n):
+        p = lax.rem(me + o, n)
+        copy(wg_ref.at[p], w1_s.at[p], w1_sem, p, p, {"lon": p}).wait_recv()
+    w2_s[pl.ds(lat, 1)] = jnp.sum(w1_s[...].astype(F32), axis=0, keepdims=True).astype(BF16)
+    for o in range(1, lats):
+        p = lax.rem(lat + o, lats)
+        cp = copy(w2_s.at[lat], w2_s.at[lat], w2_sem, p, lat, {"lat": p})
+        cp.start()
+        sends.append(cp)
+
+    for cp, (o, j) in zip(first, order):
+        cp.wait_recv()
+
+        def add(i, _, o=o, j=j):
+            mine = gb_ref[(core * chips + j) * share + i].astype(F32)
+            total = (mine + pair_s[o, i].astype(F32)).astype(BF16)
+            if o:
+                send_s[o, i] = total
+            else:
+                recv_s[chip, i] = total
+            return 0
+
+        lax.fori_loop(0, share, add, 0)
+        if o:
+            cp2 = copy(
+                send_s.at[o], recv_s.at[chip], cross_sem, o, chip, {"lon": j * 2 + core}
+            )
+            cp2.start()
+            sends.append(cp2)
+
+    for o in range(1, lats):
+        p = lax.rem(lat + o, lats)
+        copy(w2_s.at[p], w2_s.at[p], w2_sem, p, p, {"lat": p}).wait_recv()
+    wout_ref[pl.ds(me, 1)] = jnp.sum(w2_s[...].astype(F32), axis=0, keepdims=True).astype(BF16)
+    for o in range(1, n):
+        p = lax.rem(me + o, n)
+        cp = copy(wout_ref.at[me], wout_ref.at[me], w3_sem, p, me, {"lon": p})
+        cp.start()
+        sends.append(cp)
+
+    for o in range(1, chips):
+        j = lax.rem(chip + o, chips)
+        copy(send_s.at[o], recv_s.at[j], cross_sem, o, j, {"lon": j * 2 + core}).wait_recv()
+
+    def total(i, _):
+        acc = recv_s[0, i].astype(F32)
+        for j in range(1, chips):
+            acc = acc + recv_s[j, i].astype(F32)
+        out_ref[(core * chips + chip) * share + i] = acc.astype(BF16)
+        return 0
+
+    lax.fori_loop(0, share, total, 0)
+    own = out_ref.at[piece(core, chip)]
+    for o in range(1, chips):
+        j = lax.rem(chip + o, chips)
+        cp = copy(own, own, back_sem, j, chip, {"lon": j * 2 + core})
+        cp.start()
+        sends.append(cp)
+    cp = copy(own, own, fwd_sem, chip, chip, {"lon": partner})
+    cp.start()
+    sends.append(cp)
+    for o in range(1, chips):
+        j = lax.rem(chip + o, chips)
+        part = out_ref.at[piece(core, j)]
+        copy(part, part, back_sem, j, j, {"lon": j * 2 + core}).wait_recv()
+        cp = copy(part, part, fwd_sem, j, j, {"lon": partner})
+        cp.start()
+        sends.append(cp)
+    for j in range(chips):
+        part = out_ref.at[piece(other, j)]
+        copy(part, part, fwd_sem, j, j, {"lon": partner}).wait_recv()
+    for o in range(1, n):
+        p = lax.rem(me + o, n)
+        copy(wout_ref.at[p], wout_ref.at[p], w3_sem, p, p, {"lon": p}).wait_recv()
+    for cp in sends:
+        cp.wait_send()
+
+
+def reduce_all(gbias, weights):
+    n, lats = lax.axis_size("lon"), lax.axis_size("lat")
+    chips = n // 2
+    types, packed, lanes = gbias.shape
+    rows, width = weights.shape
+    share = types // n
+    weights = weights.reshape(n, rows // n, width)
+    vm = pl.BlockSpec(memory_space=pltpu.VMEM)
+    sem = lambda k: pltpu.SemaphoreType.DMA((2, k))
+    block = pltpu.VMEM((chips, share, packed, lanes), BF16)
+    out, wout = pl.pallas_call(
+        functools.partial(reduce_kernel, n, lats),
+        in_specs=[vm, vm],
+        out_specs=[vm, vm],
+        out_shape=[
+            jax.ShapeDtypeStruct(gbias.shape, BF16),
+            jax.ShapeDtypeStruct(weights.shape, BF16),
+        ],
+        scratch_shapes=[
+            block,
+            block,
+            block,
+            pltpu.VMEM((n, rows // n, width), BF16),
+            pltpu.VMEM((lats, rows // n, width), BF16),
+            sem(chips),
+            sem(chips),
+            sem(chips),
+            sem(chips),
+            sem(n),
+            sem(lats),
+            sem(n),
+        ],
+        compiler_params=pltpu.CompilerParams(
+            collective_id=0, has_side_effects=True, vmem_limit_bytes=40 * 2**20
+        ),
+        cost_estimate=pl.CostEstimate(
+            flops=30_000_000_000, bytes_accessed=60_000_000, transcendentals=0
+        ),
+    )(gbias, weights)
+    return out, wout.reshape(rows, width)
+
+
 def window_call(chunk, last, perm, frame_in, frame_cot, weight_qkv, weight_proj, bias):
     levels, height, wide, channels = frame_in.shape
     level_windows = levels // WIN_Z
@@ -257,35 +432,28 @@
     columns = jnp.arange(WIN_Z * WIN_LAT * wide, dtype=jnp.int32)
     perm = (source[:, None] == columns[None, :]).astype(BF16)
 
-    frames, qkv, proj, biases = [], 0.0, 0.0, []
-    for chunk in range(CHUNKS):
-        gframe, gqkv, gproj, gbias = window_call(
-            chunk, last, perm, frame_in, frame_cot, weight_qkv, weight_proj, bias
-        )
-        frames.append(gframe)
-        qkv = qkv + gqkv
-        proj = proj + gproj
-        biases.append(lax.psum(gbias, "lon"))
-
-    gwide = jnp.roll(jnp.concatenate(frames, axis=1), WIN_Z // 2, axis=0)
+    gframe, gqkv, gproj, gbias = window_call(
+        0, last, perm, frame_in, frame_cot, weight_qkv, weight_proj, bias
+    )
+    weights = jnp.concatenate([gqkv, gproj], axis=1).astype(BF16)
+    packed, weights = reduce_all(gbias, weights)
+    weights = weights.astype(F32)
+
+    gwide = jnp.roll(gframe, WIN_Z // 2, axis=0)
     side = ring_permute(gwide[:, :, breadth:], "lon", 1)
     seam = jnp.concatenate(
         [gwide[:, :, :HALO] + side, gwide[:, :, HALO:breadth]], axis=2
     )
     down = line_permute(seam[:, height - lat_shift :], "lat", 1)
     input_grad = jnp.concatenate([down, seam[:, : height - lat_shift]], axis=1)
-    qkv_grad, proj_grad = lax.psum((qkv.astype(BF16), proj.astype(BF16)), ("lat", "lon"))
 
     stack = HEADS * WTOK
-    outs = []
-    for packed in biases:
-        kinds = packed.shape[0]
-        head = packed[:, :stack].reshape(kinds, HEADS, WTOK, LANES)
-        tail = packed[:, stack:, : HEADS * TAIL].reshape(kinds, WTOK, HEADS, TAIL)
-        both = jnp.concatenate([head, tail.transpose(0, 2, 1, 3)], axis=3)
-        outs.append(both.astype(F32).reshape(kinds, HEADS, WTOK * WTOK))
-    bias_grad = jnp.concatenate(outs, axis=0)
-    return input_grad, qkv_grad.astype(F32), proj_grad.astype(F32), bias_grad
+    kinds = packed.shape[0]
+    head = packed[:, :stack].reshape(kinds, HEADS, WTOK, LANES)
+    tail = packed[:, stack:, : HEADS * TAIL].reshape(kinds, WTOK, HEADS, TAIL)
+    both = jnp.concatenate([head, tail.transpose(0, 2, 1, 3)], axis=3)
+    bias_grad = both.astype(F32).reshape(kinds, HEADS, WTOK * WTOK)
+    return input_grad, weights[:, : 3 * channels], weights[:, 3 * channels :], bias_grad
 
 
 def solution(mesh):

time: 423 us -> 272 us (0.64)
  waiting for transfers between devices: 217 us -> 13.1 us
  Pallas kernels: 101 us -> 163 us
  between operations: 14.3 us -> 0.89 us
  local copies, waits for them, and re-layouts: 55.2 us -> 63.3 us
    psum x2 -> x0, waiting for transfers between devices: 190 us -> none  [the longest x1 111 us: local(): lax.psum((qkv.astype(BF16), proj.astype(BF16)), ('lat', 'lon'))]
    pallas_call x0 -> x1, Pallas kernels: none -> 64.1 us  [reduce_all(): pl.pallas_call(functools.partial(reduce_kernel, n, lats), in_specs=[vm, v...]
    ppermute x3, waiting for transfers between devices: 25.6 us -> 13.1 us  [ring_permute(): lax.ppermute(block, axis, [((i - distance) % size, i) for i in range(size)])]
    concatenate x3 -> x1, other arithmetic: 9.48 us -> 0.1 us  [local(): weights = jnp.concatenate([gqkv, gproj], axis=1).astype(BF16)]
    convert_element_type x4 -> x2, local copies, waits for them, and re-layouts: 17.7 us -> 24.4 us  [local(): bias_grad = both.astype(F32).reshape(kinds, HEADS, WTOK * WTOK)]
    convert_element_type x4 -> x2, other arithmetic: 4.74 us -> 10.3 us  [the longest x1 10.2 us: local(): bias_grad = both.astype(F32).reshape(kinds, HEADS, WTOK * WTOK)]
    pallas_call x2 -> x1, Pallas kernels: 101 us -> 98.8 us  [window_call(): pl.pallas_call(functools.partial(kernel, first, lat_windows, level_window...]
  transfers between devices with their start and end apart: 8 -> 6, of which waited for: 5 -> 2; matrix products, arithmetic and copies ran while one was open for 8% -> 25% of each run, Pallas kernels for 0% -> 0%
where the time goes in v2:
time: 272 us
  Pallas kernels  163 us (60%)
  local copies, waits for them, and re-layouts  63.3 us (23%)
  other arithmetic  21.9 us (8%)
  waiting for transfers between devices  13.1 us (5%)
  starting transfers between devices  9.62 us (4%)
    pallas_call x1, Pallas kernels, window_call(): pl.pallas_call(functools.partial(kernel, first, lat_windows, level_window...  98.8 us
    pallas_call x1, Pallas kernels, reduce_all(): pl.pallas_call(functools.partial(reduce_kernel, n, lats), in_specs=[vm, v...  64.1 us
    convert_element_type x2, local copies, waits for them, and re-layouts, local(): bias_grad = both.astype(F32).reshape(kinds, HEADS, WTOK * WTOK)  24.4 us
    reshape x1, local copies, waits for them, and re-layouts, local(): bias = bias_table.reshape(types_local, HEADS * WTOK, WTOK)  13.8 us
    ppermute x3, waiting for transfers between devices, ring_permute(): lax.ppermute(block, axis, [((i - distance) % size, i) for i in range(size)])  13.1 us
    convert_element_type x1, other arithmetic, local(): bias_grad = both.astype(F32).reshape(kinds, HEADS, WTOK * WTOK)  10.2 us
    unnamed x19, local copies, waits for them, and re-layouts  5.82 us
  transfers between devices with their start and end apart: 6, of which 2 were waited for; matrix products, arithmetic and copies ran while one was open for 25% of the time, Pallas kernels for 0%

profile of v2, /device:TPU:0, one launch (start us, length us, event | category | flops | bytes accessed | tf_op | source)
XLA Modules:
  0.0 271.6 jit_solution(16332065964760047950)
XLA Ops:
  0.6 1.3 slice.56
  2.0 3.4 %collective-permute-start.2 = (bf16[8,24,8,192]{3,2,1,0:T(8,128)(2,1)S(1)}, bf16[8,24,8,192]{3,2,1,0:T(8,128)(2,1)S(1)}, u32[]{:S(2)}, u32[]{:S(2)}) collective-permute-start(bf16[8,24,8,192]{3,2,1,0:T(8,128)(2,1)S(1)} %slice.56), channel_id=1, source_target_pairs={{4,0},{8,4},{12,8},{16,12},{20,16},{24,20},{28,24},{0,28},{5,1},{9... | collective-permute-start | bytes 1769480 | tf_op jit(solution)/shard_map/ppermute | solution.py:27
  5.4 1.2 slice.53
  6.6 0.7 collective-permute-start
  8.0 6.9 %collective-permute-done.2 = bf16[8,24,8,192]{3,2,1,0:T(8,128)(2,1)S(1)} collective-permute-done((bf16[8,24,8,192]{3,2,1,0:T(8,128)(2,1)S(1)}, bf16[8,24,8,192]{3,2,1,0:T(8,128)(2,1)S(1)}, u32[]{:S(2)}, u32[]{:S(2)}) %collective-permute-start.2) | collective-permute-done | bytes 589856 | tf_op jit(solution)/shard_map/ppermute | solution.py:27
  15.0 0.9 slice.73
  15.9 1.3 collective-permute-start.3
  17.2 6.2 %collective-permute-done = bf16[8,24,8,192]{3,2,1,0:T(8,128)(2,1)S(1)} collective-permute-done((bf16[8,24,8,192]{3,2,1,0:T(8,128)(2,1)S(1)}, bf16[8,24,8,192]{3,2,1,0:T(8,128)(2,1)S(1)}, u32[]{:S(2)}, u32[]{:S(2)}) %collective-permute-start) | collective-permute-done | bytes 589856 | tf_op jit(solution)/shard_map/ppermute | solution.py:27
  23.4 0.8 slice.71
  24.2 1.3 collective-permute-start.1
  25.6 3.5 %copy.12 = bf16[16,6,20736]{2,1,0:T(8,128)(2,1)} copy(bf16[16,6,20736]{2,0,1:T(8,128)(2,1)S(1)} %copy-done.7) | data formatting | bytes 7962624 | tf_op args[4]
  29.2 13.8 %reshape.86.bias_ref = bf16[16,864,144]{2,1,0:T(8,128)(2,1)} reshape(bf16[16,6,20736]{2,1,0:T(8,128)(2,1)} %copy.12) | data formatting | bytes 7962624 | tf_op jit(solution)/shard_map/reshape | solution.py:420
  43.0 2.1 slice.72
  45.4 3.2 %pad_maximum_fusion.1.ca_ref.cb_ref = bf16[8,24,32,192]{3,2,1,0:T(8,128)(2,1)} fusion(bf16[8,3,32,192]{3,2,1,0:T(8,128)(2,1)} %collective-permute-done.3, bf16[8,21,32,192]{3,2,1,0:T(8,128)(2,1)S(1)} %slice.72), kind=kLoop, calls=%fused_computation.5 | loop fusion | flops 1179648 | bytes 4718592 | tf_op jit(solution)/shard_map/concatenate | solution.py:418
  48.6 3.3 %pad_maximum_fusion.xa_ref.xb_ref = bf16[8,24,32,192]{3,2,1,0:T(8,128)(2,1)} fusion(bf16[8,3,32,192]{3,2,1,0:T(8,128)(2,1)} %collective-permute-done.1, bf16[8,21,32,192]{3,2,1,0:T(8,128)(2,1)S(1)} %slice.70), kind=kLoop, calls=%fused_computation.4 | loop fusion | flops 1179648 | bytes 4718592 | tf_op jit(solution)/shard_map/concatenate | solution.py:417
  51.8 98.8 %shard_map.84 = (bf16[8,24,32,192]{3,2,1,0:T(8,128)(2,1)S(1)}, f32[192,576]{1,0:T(8,128)S(1)}, f32[192,192]{1,0:T(8,128)S(1)}, bf16[16,1008,128]{2,1,0:T(8,128)(2,1)}) custom-call(s32[1]{0:T(128)} %bitcast.last_ref, bf16[288,384]{1,0:T(8,128)(2,1)S(1)} %fusion.4.perm_ref, bf16[8,24,32,192]{3,2,1,0:T(8,128)(2,1)} %pad_maximum_fusion.xa_ref.xb_ref, ...), custom_call_target="tpu_custom_call" | custom-call | flops 24000000000 | bytes 32000000 | tf_op jit(solution)/shard_map/pallas_call | solution.py:358
  151.1 1.6 copy-done.2
  152.8 64.1 %shard_map.85 = (bf16[16,1008,128]{2,1,0:T(8,128)(2,1)S(1)}, bf16[8,24,768]{2,1,0:T(8,128)(2,1)S(1)}) custom-call(bf16[16,1008,128]{2,1,0:T(8,128)(2,1)S(1)} %copy-done.2, bf16[8,24,768]{2,1,0:T(8,128)(2,1)S(1)} %pad_maximum_fusion.4.wg_ref), custom_call_target="tpu_custom_call" | custom-call | flops 30000001024 | bytes 60000000 | tf_op jit(solution)/shard_map/pallas_call | solution.py:306
  216.9 0.9 slice.69
  217.8 2.0 slice.68
  219.7 1.1 pad_maximum_fusion.3
  221.3 2.3 copy.13
  223.6 3.9 %copy.14 = bf16[16,6,144,16]{3,2,1,0:T(8,128)(2,1)} copy(bf16[16,6,144,16]{2,3,1,0:T(8,128)(2,1)} %bitcast.13) | data formatting | bytes 884736 | tf_op jit(solution)/shard_map/transpose | solution.py:454
  227.5 10.2 %maximum_convert_fusion = f32[16,6,144,144]{3,2,1,0:T(8,128)} fusion(bf16[16,6,144,16]{3,2,1,0:T(8,128)(2,1)} %copy.14, bf16[16,6,144,128]{3,2,1,0:T(8,128)(2,1)} %bitcast.12), kind=kLoop, calls=%fused_computation | loop fusion | flops 7962624 | bytes 11943936 | tf_op jit(solution)/shard_map/convert_element_type | solution.py:455
  237.7 1.4 maximum_add_fusion
  239.7 2.5 collective-permute-start.5
  242.3 0.8 slice.76
  243.1 0.8 slice.77
  243.9 14.5 %reshape.93 = f32[16,6,20736]{2,1,0:T(8,128)} reshape(f32[16,6,144,144]{3,2,1,0:T(8,128)} %maximum_convert_fusion) | data formatting | bytes 15925248 | tf_op jit(solution)/shard_map/convert_element_type | solution.py:455
  258.5 9.8 %copy.16 = f32[16,6,20736]{2,0,1:T(8,128)} copy(f32[16,6,20736]{2,1,0:T(8,128)} %reshape.93) | data formatting | bytes 15925248 | tf_op jit(solution)/shard_map/convert_element_type | solution.py:455
  268.3 1.6 slice-done
  269.9 1.8 pad_maximum_fusion.2
  (36 shorter events, 2.8 us)
Async XLA Ops:
  0.6 6.7 %copy-start.5 = (bf16[8,24,24,192]{3,2,1,0:T(8,128)(2,1)S(1)}, bf16[8,24,24,192]{3,2,1,0:T(8,128)(2,1)}, u32[]{:S(2)}) copy-start(bf16[8,24,24,192]{3,2,1,0:T(8,128)(2,1)} %param.6) | copy-start | bytes 5308420
  2.0 5.7 %copy-start.6 = (bf16[8,24,24,192]{3,2,1,0:T(8,128)(2,1)S(1)}, bf16[8,24,24,192]{3,2,1,0:T(8,128)(2,1)}, u32[]{:S(2)}) copy-start(bf16[8,24,24,192]{3,2,1,0:T(8,128)(2,1)} %param.5) | copy-start | bytes 5308420
  2.0 12.9 %collective-permute-start.2 = (bf16[8,24,8,192]{3,2,1,0:T(8,128)(2,1)S(1)}, bf16[8,24,8,192]{3,2,1,0:T(8,128)(2,1)S(1)}, u32[]{:S(2)}, u32[]{:S(2)}) collective-permute-start(bf16[8,24,8,192]{3,2,1,0:T(8,128)(2,1)S(1)} %slice.56), channel_id=1, source_target_pairs={{4,0},{8,4},{12,8},{16,12},{20,16},{24,20},{28,24},{0,28},{5,1},{9... | collective-permute-start | bytes 1769480 | tf_op jit(solution)/shard_map/ppermute | solution.py:27
  6.6 16.7 %collective-permute-start = (bf16[8,24,8,192]{3,2,1,0:T(8,128)(2,1)S(1)}, bf16[8,24,8,192]{3,2,1,0:T(8,128)(2,1)S(1)}, u32[]{:S(2)}, u32[]{:S(2)}) collective-permute-start(bf16[8,24,8,192]{3,2,1,0:T(8,128)(2,1)S(1)} %slice.53), channel_id=1, source_target_pairs={{4,0},{8,4},{12,8},{16,12},{20,16},{24,20},{28,24},{0,28},{5,1},{9... | collective-permute-start | bytes 1769480 | tf_op jit(solution)/shard_map/ppermute | solution.py:27
  8.0 17.6 %copy-start.7 = (bf16[16,6,20736]{2,0,1:T(8,128)(2,1)S(1)}, bf16[16,6,20736]{2,0,1:T(8,128)(2,1)}, u32[]{:S(2)}) copy-start(bf16[16,6,20736]{2,0,1:T(8,128)(2,1)} %param.9) | copy-start | bytes 11943940
  15.0 9.2 %copy-start.3 = (bf16[8,24,32,192]{3,2,1,0:T(8,128)(2,1)}, bf16[8,24,32,192]{3,2,1,0:T(8,128)(2,1)S(1)}, u32[]{:S(2)}) copy-start(bf16[8,24,32,192]{3,2,1,0:T(8,128)(2,1)S(1)} %constant_dynamic-update-slice_fusion.2) | copy-start | bytes 7077892
  15.9 29.5 %collective-permute-start.3 = (bf16[8,3,32,192]{3,2,1,0:T(8,128)(2,1)}, bf16[8,3,32,192]{3,2,1,0:T(8,128)(2,1)}, u32[]{:S(2)}, u32[]{:S(2)}) collective-permute-start(bf16[8,3,32,192]{3,2,1,0:T(8,128)(2,1)} %slice.73), channel_id=1, source_target_pairs={{1,0},{2,1},{3,2},{5,4},{6,5},{7,6},{9,8},{10,9},{11,10},{13,12},{... | collective-permute-start | bytes 884744 | tf_op jit(solution)/shard_map/ppermute | solution.py:33
  24.2 24.4 %collective-permute-start.1 = (bf16[8,3,32,192]{3,2,1,0:T(8,128)(2,1)}, bf16[8,3,32,192]{3,2,1,0:T(8,128)(2,1)}, u32[]{:S(2)}, u32[]{:S(2)}) collective-permute-start(bf16[8,3,32,192]{3,2,1,0:T(8,128)(2,1)} %slice.71), channel_id=1, source_target_pairs={{1,0},{2,1},{3,2},{5,4},{6,5},{7,6},{9,8},{10,9},{11,10},{13,12},{... | collective-permute-start | bytes 884744 | tf_op jit(solution)/shard_map/ppermute | solution.py:33
  48.6 3.3 %copy-start = (bf16[192,576]{1,0:T(8,128)(2,1)S(1)}, bf16[192,576]{1,0:T(8,128)(2,1)}, u32[]{:S(2)}) copy-start(bf16[192,576]{1,0:T(8,128)(2,1)} %wqkv_ref.1) | copy-start | bytes 663556
  48.6 3.3 %copy-start.1 = (bf16[192,192]{1,0:T(8,128)(2,1)S(1)}, bf16[192,192]{1,0:T(8,128)(2,1)}, u32[]{:S(2)}) copy-start(bf16[192,192]{1,0:T(8,128)(2,1)} %wproj_ref.1) | copy-start | bytes 221188
  150.6 2.2 copy-start.2
  220.8 16.9 %collective-permute-start.4 = (bf16[8,24,8,192]{3,2,1,0:T(8,128)(2,1)}, bf16[8,24,8,192]{3,2,1,0:T(8,128)(2,1)}, u32[]{:S(2)}, u32[]{:S(2)}) collective-permute-start(bf16[8,24,8,192]{3,2,1,0:T(8,128)(2,1)} %pad_maximum_fusion.3), channel_id=1, source_target_pairs={{28,0},{0,4},{4,8},{8,12},{12,16},{16,20},{20,24},{24,28},{29,1},{... | collective-permute-start | bytes 1769480 | tf_op jit(solution)/shard_map/ppermute | solution.py:27
  239.7 2.6 copy-start.4
  239.7 28.6 %collective-permute-start.5 = (bf16[8,3,24,192]{3,2,1,0:T(8,128)(2,1)S(1)}, bf16[8,3,24,192]{3,2,1,0:T(8,128)(2,1)S(1)}, u32[]{:S(2)}, u32[]{:S(2)}) collective-permute-start(bf16[8,3,24,192]{3,2,1,0:T(8,128)(2,1)S(1)} %slice.74), channel_id=1, source_target_pairs={{0,1},{1,2},{2,3},{4,5},{5,6},{6,7},{8,9},{9,10},{10,11},{12,13},{... | collective-permute-start | bytes 663560 | tf_op jit(solution)/shard_map/ppermute | solution.py:33
  268.3 1.6 slice-start

commit v3 on v2

--- a/solution.py
+++ b/solution.py
@@ -335,6 +335,104 @@
     return out, wout.reshape(rows, width)
 
 
+def unpack_kernel(packed_ref, out_ref, main_s, tail_s):
+    stack = HEADS * WTOK
+    main_s[...] = packed_ref[0, :stack].astype(F32)
+    tails = packed_ref[0, stack:].astype(F32)
+    for h in range(HEADS):
+        turned = tails if h == 0 else pltpu.roll(tails, LANES - h * TAIL, 1)
+        tail_s[h * WTOK : (h + 1) * WTOK] = turned
+    group = LANES // TAIL
+    lane = lax.broadcasted_iota(jnp.int32, (HEADS, LANES), 1)
+
+    def body(m, _):
+        before_main = before_tail = None
+        for r in range(group + 1):
+            tile = None
+            if r < group:
+                at = pl.ds(m * group + r, HEADS, stride=WTOK)
+                here_main, here_tail = main_s[at, :], tail_s[at, :]
+                if r:
+                    here_main = pltpu.roll(here_main, TAIL * r, 1)
+                    here_tail = pltpu.roll(here_tail, TAIL * r, 1)
+                tile = here_main
+            if r:
+                ended = before_tail
+                if r > 1:
+                    ended = jnp.where(lane < TAIL * (r - 1), before_main, before_tail)
+                tile = ended if r == group else jnp.where(lane < TAIL * r, ended, tile)
+            start = pl.multiple_of(m * (group * WTOK) + r * LANES, LANES)
+            out_ref[0, :, pl.ds(start, LANES)] = tile
+            if r < group:
+                before_main, before_tail = here_main, here_tail
+        return 0
+
+    lax.fori_loop(0, WTOK // group, body, 0)
+
+
+def unpack(packed):
+    kinds, rows, lanes = packed.shape
+    stack = HEADS * WTOK
+    return pl.pallas_call(
+        unpack_kernel,
+        grid=(kinds,),
+        in_specs=[pl.BlockSpec((1, rows, lanes), lambda i: (i, 0, 0))],
+        out_specs=pl.BlockSpec((1, HEADS, WTOK * WTOK), lambda i: (i, 0, 0)),
+        out_shape=jax.ShapeDtypeStruct((kinds, HEADS, WTOK * WTOK), F32),
+        scratch_shapes=[pltpu.VMEM((stack, LANES), F32), pltpu.VMEM((stack, LANES), F32)],
+        cost_estimate=pl.CostEstimate(
+            flops=10_000_000_000, bytes_accessed=15_000_000, transcendentals=0
+        ),
+    )(packed)
+
+
+def spread_kernel(flat_ref, main_ref, tail_ref, main_s, tail_s):
+    group = LANES // TAIL
+    lane = lax.broadcasted_iota(jnp.int32, (HEADS, LANES), 1)
+
+    def body(m, _):
+        tiles = []
+        for r in range(group + 1):
+            start = pl.multiple_of(m * (group * WTOK) + r * LANES, LANES)
+            tiles.append(flat_ref[0, :, pl.ds(start, LANES)].astype(F32))
+        for r in range(group):
+            main, tail = tiles[r], tiles[r + 1]
+            if r:
+                main = jnp.where(lane >= TAIL * r, main, tail)
+                main = pltpu.roll(main, LANES - TAIL * r, 1)
+                tail = pltpu.roll(tail, LANES - TAIL * r, 1)
+            at = pl.ds(m * group + r, HEADS, stride=WTOK)
+            main_s[at, :] = main
+            tail_s[at, :] = tail
+        return 0
+
+    lax.fori_loop(0, WTOK // group, body, 0)
+    main_ref[0] = main_s[...].astype(BF16)
+    tail_ref[0] = tail_s[:, :TAIL].astype(BF16)
+
+
+def spread_whole(flat_ref, out_ref, main_s, tail_s):
+    spread_kernel(
+        flat_ref, out_ref.at[:, :, :LANES], out_ref.at[:, :, LANES:], main_s, tail_s
+    )
+
+
+def spread(table):
+    kinds = table.shape[0]
+    stack = HEADS * WTOK
+    return pl.pallas_call(
+        spread_whole,
+        grid=(kinds,),
+        in_specs=[pl.BlockSpec((1, HEADS, WTOK * WTOK), lambda i: (i, 0, 0))],
+        out_specs=pl.BlockSpec((1, stack, WTOK), lambda i: (i, 0, 0)),
+        out_shape=jax.ShapeDtypeStruct((kinds, stack, WTOK), BF16),
+        scratch_shapes=[pltpu.VMEM((stack, LANES), F32), pltpu.VMEM((stack, LANES), F32)],
+        cost_estimate=pl.CostEstimate(
+            flops=10_000_000_000, bytes_accessed=15_000_000, transcendentals=0
+        ),
+    )(table)
+
+
 def window_call(chunk, last, perm, frame_in, frame_cot, weight_qkv, weight_proj, bias):
     levels, height, wide, channels = frame_in.shape
     level_windows = levels // WIN_Z
@@ -405,10 +503,7 @@
     levels, height, breadth, channels = normed.shape
     lat_shift = WIN_LAT // 2
     lon_shift = WIN_LON // 2
-    level_windows = levels // WIN_Z
-    lat_windows = height // WIN_LAT
     lon_windows = breadth // WIN_LON
-    types_local = level_windows * lat_windows
     wide = breadth + HALO
     across = ring_permute((normed[:, :, :HALO], cotangent[:, :, :HALO]), "lon", -1)
     wide_in = jnp.concatenate([normed, across[0]], axis=2)
@@ -417,7 +512,7 @@
     frame_in = jnp.concatenate([wide_in[:, lat_shift:], upward[0]], axis=1)
     frame_cot = jnp.concatenate([wide_cot[:, lat_shift:], upward[1]], axis=1)
     last = (lax.axis_index("lat") == lax.axis_size("lat") - 1).astype(jnp.int32).reshape(1)
-    bias = bias_table.reshape(types_local, HEADS * WTOK, WTOK)
+    bias = spread(bias_table)
 
     rows = jnp.arange(lon_windows * WTOK, dtype=jnp.int32)
     token = rows % WTOK
@@ -447,12 +542,7 @@
     down = line_permute(seam[:, height - lat_shift :], "lat", 1)
     input_grad = jnp.concatenate([down, seam[:, : height - lat_shift]], axis=1)
 
-    stack = HEADS * WTOK
-    kinds = packed.shape[0]
-    head = packed[:, :stack].reshape(kinds, HEADS, WTOK, LANES)
-    tail = packed[:, stack:, : HEADS * TAIL].reshape(kinds, WTOK, HEADS, TAIL)
-    both = jnp.concatenate([head, tail.transpose(0, 2, 1, 3)], axis=3)
-    bias_grad = both.astype(F32).reshape(kinds, HEADS, WTOK * WTOK)
+    bias_grad = unpack(packed)
     return input_grad, weights[:, : 3 * channels], weights[:, 3 * channels :], bias_grad
 
 

time: 272 us -> 286 us (1.051)
  Pallas kernels: 163 us -> 222 us
  local copies, waits for them, and re-layouts: 63.3 us -> 29.1 us
  other arithmetic: 21.9 us -> 11.8 us
    pallas_call x0 -> x2, Pallas kernels: none -> 57.1 us  [the longest x1 29.1 us: unpack(): pl.pallas_call(unpack_kernel, grid=(kinds,), in_specs=[pl.BlockSpec((1, r...]
    convert_element_type x2 -> x0, local copies, waits for them, and re-layouts: 24.4 us -> none  [local(): bias_grad = both.astype(F32).reshape(kinds, HEADS, WTOK * WTOK)]
    reshape x1 -> x0, local copies, waits for them, and re-layouts: 13.8 us -> none  [local(): bias = bias_table.reshape(types_local, HEADS * WTOK, WTOK)]
    ppermute x3, waiting for transfers between devices: 13.1 us -> 0.01 us  [ring_permute(): lax.ppermute(block, axis, [((i - distance) % size, i) for i in range(size)])]
    ppermute x3, waiting for transfers between devices: 0.01 us -> 11.3 us  [line_permute(): return lax.ppermute(block, axis, route)]
    unnamed x19 -> x20, local copies, waits for them, and re-layouts: 5.82 us -> 16.4 us
    convert_element_type x1 -> x0, other arithmetic: 10.2 us -> none  [local(): bias_grad = both.astype(F32).reshape(kinds, HEADS, WTOK * WTOK)]
    slice x3 -> x0, local copies, waits for them, and re-layouts: 5.11 us -> none  [the longest x2 3.15 us: local(): tail = packed[:, stack:, :HEADS * TAIL].reshape(kinds, WTOK, HEADS, TAIL)]
  transfers between devices with their start and end apart: 6 -> 6, of which waited for: 2 -> 2; matrix products, arithmetic and copies ran while one was open for 25% -> 9% of each run, Pallas kernels for 0% -> 43%
where the time goes in v3:
time: 286 us; the launch traced here: 285 us
  Pallas kernels  222 us (78%)
  local copies, waits for them, and re-layouts  29.1 us (10%)
  other arithmetic  11.8 us (4%)
  waiting for transfers between devices  11.3 us (4%)
  starting transfers between devices  10.5 us (4%)
    pallas_call x1, Pallas kernels, window_call(): pl.pallas_call(functools.partial(kernel, first, lat_windows, level_window...  98.8 us
    pallas_call x1, Pallas kernels, reduce_all(): pl.pallas_call(functools.partial(reduce_kernel, n, lats), in_specs=[vm, v...  66.1 us
    pallas_call x1, Pallas kernels, unpack(): pl.pallas_call(unpack_kernel, grid=(kinds,), in_specs=[pl.BlockSpec((1, r...  29.1 us
    pallas_call x1, Pallas kernels, spread(): pl.pallas_call(spread_whole, grid=(kinds,), in_specs=[pl.BlockSpec((1, HE...  28 us
    unnamed x20, local copies, waits for them, and re-layouts  16.4 us
    ppermute x3, waiting for transfers between devices, line_permute(): return lax.ppermute(block, axis, route)  11.3 us
    ppermute x3, starting transfers between devices, line_permute(): return lax.ppermute(block, axis, route)  6.5 us
  transfers between devices with their start and end apart: 6, of which 2 were waited for; matrix products, arithmetic and copies ran while one was open for 9% of the time, Pallas kernels for 43%

profile of v3, /device:TPU:0, one launch (start us, length us, event | category | flops | bytes accessed | tf_op | source)
XLA Modules:
  0.0 285.5 jit_solution(1093831435166317679)
XLA Ops:
  0.6 2.1 slice.50
  2.7 3.4 %collective-permute-start.2 = (bf16[8,24,8,192]{3,2,1,0:T(8,128)(2,1)}, bf16[8,24,8,192]{3,2,1,0:T(8,128)(2,1)}, u32[]{:S(2)}, u32[]{:S(2)}) collective-permute-start(bf16[8,24,8,192]{3,2,1,0:T(8,128)(2,1)} %slice.50), channel_id=1, source_target_pairs={{4,0},{8,4},{12,8},{16,12},{20,16},{24,20},{28,24},{0,28},{5,1},{9... | collective-permute-start | bytes 1769480 | tf_op jit(solution)/shard_map/ppermute | solution.py:27
  6.1 2.1 slice.47
  8.1 0.7 collective-permute-start
  8.8 5.6 %copy.9.flat_ref = bf16[16,6,20736]{2,1,0:T(8,128)(2,1)} copy(bf16[16,6,20736]{2,0,1:T(8,128)(2,1)} %param.9) | data formatting | bytes 7962624 | tf_op args[4]
  14.5 28.0 %shard_map.84.bias_ref = bf16[16,864,144]{2,1,0:T(8,128)(2,1)} custom-call(bf16[16,6,20736]{2,1,0:T(8,128)(2,1)} %copy.9.flat_ref), custom_call_target="tpu_custom_call" | custom-call | flops 10000000000 | bytes 15000000 | tf_op jit(solution)/shard_map/pallas_call | solution.py:423
  42.8 1.3 copy-done.7
  44.4 1.2 constant_dynamic-update-slice_fusion
  45.7 0.8 slice.63
  46.5 1.3 collective-permute-start.1
  47.8 1.2 constant_dynamic-update-slice_fusion.2
  49.1 0.8 slice.65
  49.8 1.3 collective-permute-start.3
  51.3 2.0 slice.62
  53.6 7.1 %collective-permute-done.1 = bf16[8,3,32,192]{3,2,1,0:T(8,128)(2,1)} collective-permute-done((bf16[8,3,32,192]{3,2,1,0:T(8,128)(2,1)}, bf16[8,3,32,192]{3,2,1,0:T(8,128)(2,1)}, u32[]{:S(2)}, u32[]{:S(2)}) %collective-permute-start.1) | collective-permute-done | bytes 294944 | tf_op jit(solution)/shard_map/ppermute | solution.py:33
  60.7 3.2 %pad_maximum_fusion.xa_ref.xb_ref = bf16[8,24,32,192]{3,2,1,0:T(8,128)(2,1)} fusion(bf16[8,3,32,192]{3,2,1,0:T(8,128)(2,1)} %collective-permute-done.1, bf16[8,21,32,192]{3,2,1,0:T(8,128)(2,1)S(1)} %slice.62), kind=kLoop, calls=%fused_computation.3 | loop fusion | flops 1179648 | bytes 4718592 | tf_op jit(solution)/shard_map/concatenate | solution.py:512
  63.9 4.1 %collective-permute-done.3 = bf16[8,3,32,192]{3,2,1,0:T(8,128)(2,1)} collective-permute-done((bf16[8,3,32,192]{3,2,1,0:T(8,128)(2,1)}, bf16[8,3,32,192]{3,2,1,0:T(8,128)(2,1)}, u32[]{:S(2)}, u32[]{:S(2)}) %collective-permute-start.3) | collective-permute-done | bytes 294944 | tf_op jit(solution)/shard_map/ppermute | solution.py:33
  68.0 3.2 %pad_maximum_fusion.1.ca_ref.cb_ref = bf16[8,24,32,192]{3,2,1,0:T(8,128)(2,1)} fusion(bf16[8,3,32,192]{3,2,1,0:T(8,128)(2,1)} %collective-permute-done.3, bf16[8,21,32,192]{3,2,1,0:T(8,128)(2,1)S(1)} %slice.64), kind=kLoop, calls=%fused_computation.4 | loop fusion | flops 1179648 | bytes 4718592 | tf_op jit(solution)/shard_map/concatenate | solution.py:513
  71.2 98.8 %shard_map.85 = (bf16[8,24,32,192]{3,2,1,0:T(8,128)(2,1)S(1)}, f32[192,576]{1,0:T(8,128)S(1)}, f32[192,192]{1,0:T(8,128)S(1)}, bf16[16,1008,128]{2,1,0:T(8,128)(2,1)}) custom-call(s32[1]{0:T(128)} %bitcast.last_ref, bf16[288,384]{1,0:T(8,128)(2,1)S(1)} %fusion.4.perm_ref, bf16[8,24,32,192]{3,2,1,0:T(8,128)(2,1)} %pad_maximum_fusion.xa_ref.xb_ref, ...), custom_call_target="tpu_custom_call" | custom-call | flops 24000000000 | bytes 32000000 | tf_op jit(solution)/shard_map/pallas_call | solution.py:456
  170.0 0.3 slice.54
  170.4 1.1 pad_maximum_fusion.3
  171.6 1.2 copy-done.3
  172.8 66.1 %shard_map.86 = (bf16[16,1008,128]{2,1,0:T(8,128)(2,1)S(1)}, bf16[8,24,768]{2,1,0:T(8,128)(2,1)S(1)}) custom-call(bf16[16,1008,128]{2,1,0:T(8,128)(2,1)S(1)} %copy-done.3, bf16[8,24,768]{2,1,0:T(8,128)(2,1)S(1)} %pad_maximum_fusion.4.wg_ref), custom_call_target="tpu_custom_call" | custom-call | flops 30000001024 | bytes 60000000 | tf_op jit(solution)/shard_map/pallas_call | solution.py:306
  238.9 2.0 copy-done.2
  240.9 29.1 %shard_map.87 = f32[16,6,20736]{2,1,0:T(8,128)} custom-call(bf16[16,1008,128]{2,1,0:T(8,128)(2,1)} %copy-done.2), custom_call_target="tpu_custom_call" | custom-call | flops 10000000000 | bytes 15000000 | tf_op jit(solution)/shard_map/pallas_call | solution.py:376
  270.0 1.6 maximum_add_fusion
  271.6 0.6 fusion.3
  272.2 3.9 %collective-permute-start.5 = (bf16[8,3,24,192]{3,2,1,0:T(8,128)(2,1)S(1)}, bf16[8,3,24,192]{3,2,1,0:T(8,128)(2,1)S(1)}, u32[]{:S(2)}, u32[]{:S(2)}) collective-permute-start(bf16[8,3,24,192]{3,2,1,0:T(8,128)(2,1)S(1)} %slice.66), channel_id=1, source_target_pairs={{0,1},{1,2},{2,3},{4,5},{5,6},{6,7},{8,9},{9,10},{10,11},{12,13},{... | collective-permute-start | bytes 663560 | tf_op jit(solution)/shard_map/ppermute | solution.py:33
  276.2 0.8 slice.69
  277.0 0.8 slice.68
  277.8 5.7 %copy.10 = f32[16,6,20736]{2,0,1:T(8,128)} copy(f32[16,6,20736]{2,1,0:T(8,128)S(1)} %copy-done.4) | data formatting | bytes 15925248
  283.7 1.8 pad_maximum_fusion.2
  (30 shorter events, 1.4 us)
Async XLA Ops:
  2.7 45.1 %collective-permute-start.2 = (bf16[8,24,8,192]{3,2,1,0:T(8,128)(2,1)}, bf16[8,24,8,192]{3,2,1,0:T(8,128)(2,1)}, u32[]{:S(2)}, u32[]{:S(2)}) collective-permute-start(bf16[8,24,8,192]{3,2,1,0:T(8,128)(2,1)} %slice.50), channel_id=1, source_target_pairs={{4,0},{8,4},{12,8},{16,12},{20,16},{24,20},{28,24},{0,28},{5,1},{9... | collective-permute-start | bytes 1769480 | tf_op jit(solution)/shard_map/ppermute | solution.py:27
  8.1 36.3 %collective-permute-start = (bf16[8,24,8,192]{3,2,1,0:T(8,128)(2,1)}, bf16[8,24,8,192]{3,2,1,0:T(8,128)(2,1)}, u32[]{:S(2)}, u32[]{:S(2)}) collective-permute-start(bf16[8,24,8,192]{3,2,1,0:T(8,128)(2,1)} %slice.47), channel_id=1, source_target_pairs={{4,0},{8,4},{12,8},{16,12},{20,16},{24,20},{28,24},{0,28},{5,1},{9... | collective-permute-start | bytes 1769480 | tf_op jit(solution)/shard_map/ppermute | solution.py:27
  14.5 28.0 %copy-start.6 = (bf16[8,24,24,192]{3,2,1,0:T(8,128)(2,1)S(1)}, bf16[8,24,24,192]{3,2,1,0:T(8,128)(2,1)}, u32[]{:S(2)}) copy-start(bf16[8,24,24,192]{3,2,1,0:T(8,128)(2,1)} %param.5) | copy-start | bytes 5308420
  42.4 1.7 copy-start.7
  45.7 4.2 %copy-start.5 = (bf16[8,24,32,192]{3,2,1,0:T(8,128)(2,1)}, bf16[8,24,32,192]{3,2,1,0:T(8,128)(2,1)S(1)}, u32[]{:S(2)}) copy-start(bf16[8,24,32,192]{3,2,1,0:T(8,128)(2,1)S(1)} %constant_dynamic-update-slice_fusion) | copy-start | bytes 7077892
  46.5 14.2 %collective-permute-start.1 = (bf16[8,3,32,192]{3,2,1,0:T(8,128)(2,1)}, bf16[8,3,32,192]{3,2,1,0:T(8,128)(2,1)}, u32[]{:S(2)}, u32[]{:S(2)}) collective-permute-start(bf16[8,3,32,192]{3,2,1,0:T(8,128)(2,1)} %slice.63), channel_id=1, source_target_pairs={{1,0},{2,1},{3,2},{5,4},{6,5},{7,6},{9,8},{10,9},{11,10},{13,12},{... | collective-permute-start | bytes 884744 | tf_op jit(solution)/shard_map/ppermute | solution.py:33
  49.8 18.2 %collective-permute-start.3 = (bf16[8,3,32,192]{3,2,1,0:T(8,128)(2,1)}, bf16[8,3,32,192]{3,2,1,0:T(8,128)(2,1)}, u32[]{:S(2)}, u32[]{:S(2)}) collective-permute-start(bf16[8,3,32,192]{3,2,1,0:T(8,128)(2,1)} %slice.65), channel_id=1, source_target_pairs={{1,0},{2,1},{3,2},{5,4},{6,5},{7,6},{9,8},{10,9},{11,10},{13,12},{... | collective-permute-start | bytes 884744 | tf_op jit(solution)/shard_map/ppermute | solution.py:33
  63.9 7.3 %copy-start = (bf16[192,576]{1,0:T(8,128)(2,1)S(1)}, bf16[192,576]{1,0:T(8,128)(2,1)}, u32[]{:S(2)}) copy-start(bf16[192,576]{1,0:T(8,128)(2,1)} %wqkv_ref.1) | copy-start | bytes 663556
  63.9 7.3 %copy-start.1 = (bf16[192,192]{1,0:T(8,128)(2,1)S(1)}, bf16[192,192]{1,0:T(8,128)(2,1)}, u32[]{:S(2)}) copy-start(bf16[192,192]{1,0:T(8,128)(2,1)} %wproj_ref.1) | copy-start | bytes 221188
  170.4 2.5 copy-start.3
  171.5 98.5 %collective-permute-start.4 = (bf16[8,24,8,192]{3,2,1,0:T(8,128)(2,1)}, bf16[8,24,8,192]{3,2,1,0:T(8,128)(2,1)}, u32[]{:S(2)}, u32[]{:S(2)}) collective-permute-start(bf16[8,24,8,192]{3,2,1,0:T(8,128)(2,1)} %pad_maximum_fusion.3), channel_id=1, source_target_pairs={{28,0},{0,4},{4,8},{8,12},{12,16},{16,20},{20,24},{24,28},{29,1},{... | collective-permute-start | bytes 1769480 | tf_op jit(solution)/shard_map/ppermute | solution.py:27
  238.9 2.0 copy-start.2
  270.0 7.8 %copy-start.4 = (f32[16,6,20736]{2,1,0:T(8,128)S(1)}, f32[16,6,20736]{2,1,0:T(8,128)}, u32[]{:S(2)}) copy-start(f32[16,6,20736]{2,1,0:T(8,128)} %shard_map.87) | copy-start | bytes 23887876
  272.2 11.5 %collective-permute-start.5 = (bf16[8,3,24,192]{3,2,1,0:T(8,128)(2,1)S(1)}, bf16[8,3,24,192]{3,2,1,0:T(8,128)(2,1)S(1)}, u32[]{:S(2)}, u32[]{:S(2)}) collective-permute-start(bf16[8,3,24,192]{3,2,1,0:T(8,128)(2,1)S(1)} %slice.66), channel_id=1, source_target_pairs={{0,1},{1,2},{2,3},{4,5},{5,6},{6,7},{8,9},{9,10},{10,11},{12,13},{... | collective-permute-start | bytes 663560 | tf_op jit(solution)/shard_map/ppermute | solution.py:33

commit v4 on v3

--- a/solution.py
+++ b/solution.py
@@ -17,6 +17,7 @@
 TAIL = WTOK - LANES
 HALO = 8
 CHUNKS = 1
+UNROLL = 6
 LOG2E = math.log2(math.e)
 F32 = jnp.float32
 BF16 = jnp.bfloat16
@@ -367,7 +368,12 @@
                 before_main, before_tail = here_main, here_tail
         return 0
 
-    lax.fori_loop(0, WTOK // group, body, 0)
+    def several(i, _):
+        for u in range(UNROLL):
+            body(i * UNROLL + u, 0)
+        return 0
+
+    lax.fori_loop(0, WTOK // group // UNROLL, several, 0)
 
 
 def unpack(packed):
@@ -384,53 +390,6 @@
             flops=10_000_000_000, bytes_accessed=15_000_000, transcendentals=0
         ),
     )(packed)
-
-
-def spread_kernel(flat_ref, main_ref, tail_ref, main_s, tail_s):
-    group = LANES // TAIL
-    lane = lax.broadcasted_iota(jnp.int32, (HEADS, LANES), 1)
-
-    def body(m, _):
-        tiles = []
-        for r in range(group + 1):
-            start = pl.multiple_of(m * (group * WTOK) + r * LANES, LANES)
-            tiles.append(flat_ref[0, :, pl.ds(start, LANES)].astype(F32))
-        for r in range(group):
-            main, tail = tiles[r], tiles[r + 1]
-            if r:
-                main = jnp.where(lane >= TAIL * r, main, tail)
-                main = pltpu.roll(main, LANES - TAIL * r, 1)
-                tail = pltpu.roll(tail, LANES - TAIL * r, 1)
-            at = pl.ds(m * group + r, HEADS, stride=WTOK)
-            main_s[at, :] = main
-            tail_s[at, :] = tail
-        return 0
-
-    lax.fori_loop(0, WTOK // group, body, 0)
-    main_ref[0] = main_s[...].astype(BF16)
-    tail_ref[0] = tail_s[:, :TAIL].astype(BF16)
-
-
-def spread_whole(flat_ref, out_ref, main_s, tail_s):
-    spread_kernel(
-        flat_ref, out_ref.at[:, :, :LANES], out_ref.at[:, :, LANES:], main_s, tail_s
-    )
-
-
-def spread(table):
-    kinds = table.shape[0]
-    stack = HEADS * WTOK
-    return pl.pallas_call(
-        spread_whole,
-        grid=(kinds,),
-        in_specs=[pl.BlockSpec((1, HEADS, WTOK * WTOK), lambda i: (i, 0, 0))],
-        out_specs=pl.BlockSpec((1, stack, WTOK), lambda i: (i, 0, 0)),
-        out_shape=jax.ShapeDtypeStruct((kinds, stack, WTOK), BF16),
-        scratch_shapes=[pltpu.VMEM((stack, LANES), F32), pltpu.VMEM((stack, LANES), F32)],
-        cost_estimate=pl.CostEstimate(
-            flops=10_000_000_000, bytes_accessed=15_000_000, transcendentals=0
-        ),
-    )(table)
 
 
 def window_call(chunk, last, perm, frame_in, frame_cot, weight_qkv, weight_proj, bias):
@@ -512,7 +471,7 @@
     frame_in = jnp.concatenate([wide_in[:, lat_shift:], upward[0]], axis=1)
     frame_cot = jnp.concatenate([wide_cot[:, lat_shift:], upward[1]], axis=1)
     last = (lax.axis_index("lat") == lax.axis_size("lat") - 1).astype(jnp.int32).reshape(1)
-    bias = spread(bias_table)
+    bias = bias_table.reshape(bias_table.shape[0], HEADS * WTOK, WTOK)
 
     rows = jnp.arange(lon_windows * WTOK, dtype=jnp.int32)
     token = rows % WTOK

time: 286 us -> 257 us (0.90)
  Pallas kernels: 222 us -> 181 us
  local copies, waits for them, and re-layouts: 29.1 us -> 37.4 us
    pallas_call x1 -> x0, Pallas kernels: 28 us -> none  [spread(): pl.pallas_call(spread_whole, grid=(kinds,), in_specs=[pl.BlockSpec((1, HE...]
    reshape x0 -> x1, local copies, waits for them, and re-layouts: none -> 13.8 us  [local(): bias = bias_table.reshape(bias_table.shape[0], HEADS * WTOK, WTOK)]
    pallas_call x1, Pallas kernels: 29.1 us -> 16 us  [unpack(): pl.pallas_call(unpack_kernel, grid=(kinds,), in_specs=[pl.BlockSpec((1, r...]
    ppermute x3, waiting for transfers between devices: 0.01 us -> 13.1 us  [ring_permute(): lax.ppermute(block, axis, [((i - distance) % size, i) for i in range(size)])]
    ppermute x3, waiting for transfers between devices: 11.3 us -> 0.01 us  [line_permute(): return lax.ppermute(block, axis, route)]
  transfers between devices with their start and end apart: 6 -> 6, of which waited for: 2 -> 2; matrix products, arithmetic and copies ran while one was open for 9% -> 14% of each run, Pallas kernels for 43% -> 32%
where the time goes in v4:
time: 257 us; the launch traced here: 256 us
  Pallas kernels  181 us (70%)
  local copies, waits for them, and re-layouts  37.4 us (15%)
  waiting for transfers between devices  13.1 us (5%)
  other arithmetic  11.8 us (5%)
  starting transfers between devices  11.5 us (4%)
    pallas_call x1, Pallas kernels, window_call(): pl.pallas_call(functools.partial(kernel, first, lat_windows, level_window...  98.8 us
    pallas_call x1, Pallas kernels, reduce_all(): pl.pallas_call(functools.partial(reduce_kernel, n, lats), in_specs=[vm, v...  66.6 us
    pallas_call x1, Pallas kernels, unpack(): pl.pallas_call(unpack_kernel, grid=(kinds,), in_specs=[pl.BlockSpec((1, r...  16 us
    unnamed x20, local copies, waits for them, and re-layouts  14.8 us
    reshape x1, local copies, waits for them, and re-layouts, local(): bias = bias_table.reshape(bias_table.shape[0], HEADS * WTOK, WTOK)  13.8 us
    ppermute x3, waiting for transfers between devices, ring_permute(): lax.ppermute(block, axis, [((i - distance) % size, i) for i in range(size)])  13.1 us
    ppermute x3, starting transfers between devices, line_permute(): return lax.ppermute(block, axis, route)  7.11 us
  transfers between devices with their start and end apart: 6, of which 2 were waited for; matrix products, arithmetic and copies ran while one was open for 14% of the time, Pallas kernels for 32%

profile of v4, /device:TPU:0, one launch (start us, length us, event | category | flops | bytes accessed | tf_op | source)
XLA Modules:
  0.0 256.1 jit_solution(760066687205548809)
XLA Ops:
  0.6 1.3 slice.47
  2.0 3.4 %collective-permute-start = (bf16[8,24,8,192]{3,2,1,0:T(8,128)(2,1)S(1)}, bf16[8,24,8,192]{3,2,1,0:T(8,128)(2,1)S(1)}, u32[]{:S(2)}, u32[]{:S(2)}) collective-permute-start(bf16[8,24,8,192]{3,2,1,0:T(8,128)(2,1)S(1)} %slice.47), channel_id=1, source_target_pairs={{4,0},{8,4},{12,8},{16,12},{20,16},{24,20},{28,24},{0,28},{5,1},{9... | collective-permute-start | bytes 1769480 | tf_op jit(solution)/shard_map/ppermute | solution.py:28
  5.4 1.2 slice.50
  6.6 0.7 collective-permute-start.2
  7.4 0.3 constant_dynamic-update-slice_fusion.1
  7.7 0.3 constant_dynamic-update-slice_fusion.3
  8.0 6.9 %collective-permute-done = bf16[8,24,8,192]{3,2,1,0:T(8,128)(2,1)S(1)} collective-permute-done((bf16[8,24,8,192]{3,2,1,0:T(8,128)(2,1)S(1)}, bf16[8,24,8,192]{3,2,1,0:T(8,128)(2,1)S(1)}, u32[]{:S(2)}, u32[]{:S(2)}) %collective-permute-start) | collective-permute-done | bytes 589856 | tf_op jit(solution)/shard_map/ppermute | solution.py:28
  15.0 0.8 slice.63
  15.9 1.3 collective-permute-start.1
  17.2 6.2 %collective-permute-done.2 = bf16[8,24,8,192]{3,2,1,0:T(8,128)(2,1)S(1)} collective-permute-done((bf16[8,24,8,192]{3,2,1,0:T(8,128)(2,1)S(1)}, bf16[8,24,8,192]{3,2,1,0:T(8,128)(2,1)S(1)}, u32[]{:S(2)}, u32[]{:S(2)}) %collective-permute-start.2) | collective-permute-done | bytes 589856 | tf_op jit(solution)/shard_map/ppermute | solution.py:28
  23.4 0.8 slice.65
  24.2 1.3 collective-permute-start.3
  25.6 5.6 %copy.11 = bf16[16,6,20736]{2,1,0:T(8,128)(2,1)} copy(bf16[16,6,20736]{2,0,1:T(8,128)(2,1)} %param.9) | data formatting | bytes 7962624 | tf_op args[4]
  31.3 13.8 %reshape.76.bias_ref = bf16[16,864,144]{2,1,0:T(8,128)(2,1)} reshape(bf16[16,6,20736]{2,1,0:T(8,128)(2,1)} %copy.11) | data formatting | bytes 7962624 | tf_op jit(solution)/shard_map/reshape | solution.py:474
  45.1 2.0 slice.62
  47.4 3.2 %pad_maximum_fusion.xa_ref.xb_ref = bf16[8,24,32,192]{3,2,1,0:T(8,128)(2,1)} fusion(bf16[8,3,32,192]{3,2,1,0:T(8,128)(2,1)} %collective-permute-done.1, bf16[8,21,32,192]{3,2,1,0:T(8,128)(2,1)S(1)} %slice.62), kind=kLoop, calls=%fused_computation.3 | loop fusion | flops 1179648 | bytes 4718592 | tf_op jit(solution)/shard_map/concatenate | solution.py:471
  50.6 3.3 %pad_maximum_fusion.1.ca_ref.cb_ref = bf16[8,24,32,192]{3,2,1,0:T(8,128)(2,1)} fusion(bf16[8,3,32,192]{3,2,1,0:T(8,128)(2,1)} %collective-permute-done.3, bf16[8,21,32,192]{3,2,1,0:T(8,128)(2,1)S(1)} %slice.64), kind=kLoop, calls=%fused_computation.4 | loop fusion | flops 1179648 | bytes 4718592 | tf_op jit(solution)/shard_map/concatenate | solution.py:472
  53.9 98.8 %shard_map.84 = (bf16[8,24,32,192]{3,2,1,0:T(8,128)(2,1)S(1)}, f32[192,576]{1,0:T(8,128)S(1)}, f32[192,192]{1,0:T(8,128)S(1)}, bf16[16,1008,128]{2,1,0:T(8,128)(2,1)}) custom-call(s32[1]{0:T(128)} %bitcast.last_ref, bf16[288,384]{1,0:T(8,128)(2,1)S(1)} %fusion.4.perm_ref, bf16[8,24,32,192]{3,2,1,0:T(8,128)(2,1)} %pad_maximum_fusion.xa_ref.xb_ref, ...), custom_call_target="tpu_custom_call" | custom-call | flops 24000000000 | bytes 32000000 | tf_op jit(solution)/shard_map/pallas_call | solution.py:415
  152.7 0.3 slice.54
  153.1 1.1 pad_maximum_fusion.3
  154.2 0.3 collective-permute-start.4
  154.6 0.9 copy-done.3
  155.5 66.6 %shard_map.85 = (bf16[16,1008,128]{2,1,0:T(8,128)(2,1)S(1)}, bf16[8,24,768]{2,1,0:T(8,128)(2,1)S(1)}) custom-call(bf16[16,1008,128]{2,1,0:T(8,128)(2,1)S(1)} %copy-done.3, bf16[8,24,768]{2,1,0:T(8,128)(2,1)S(1)} %pad_maximum_fusion.4.wg_ref), custom_call_target="tpu_custom_call" | custom-call | flops 30000001024 | bytes 60000000 | tf_op jit(solution)/shard_map/pallas_call | solution.py:307
  222.1 2.0 copy-done.2
  224.1 16.0 %shard_map.86 = f32[16,6,20736]{2,1,0:T(8,128)} custom-call(bf16[16,1008,128]{2,1,0:T(8,128)(2,1)} %copy-done.2), custom_call_target="tpu_custom_call" | custom-call | flops 10000000000 | bytes 15000000 | tf_op jit(solution)/shard_map/pallas_call | solution.py:382
  240.1 1.6 maximum_add_fusion
  241.7 0.6 fusion.3
  242.3 4.5 %collective-permute-start.5 = (bf16[8,3,24,192]{3,2,1,0:T(8,128)(2,1)S(1)}, bf16[8,3,24,192]{3,2,1,0:T(8,128)(2,1)S(1)}, u32[]{:S(2)}, u32[]{:S(2)}) collective-permute-start(bf16[8,3,24,192]{3,2,1,0:T(8,128)(2,1)S(1)} %slice.66), channel_id=1, source_target_pairs={{0,1},{1,2},{2,3},{4,5},{5,6},{6,7},{8,9},{9,10},{10,11},{12,13},{... | collective-permute-start | bytes 663560 | tf_op jit(solution)/shard_map/ppermute | solution.py:34
  246.9 0.8 slice.69
  247.7 0.8 slice.68
  248.5 5.7 %copy.12 = f32[16,6,20736]{2,0,1:T(8,128)} copy(f32[16,6,20736]{2,1,0:T(8,128)S(1)} %copy-done.4) | data formatting | bytes 15925248
  254.3 1.8 pad_maximum_fusion.2
  (30 shorter events, 1.0 us)
Async XLA Ops:
  0.6 6.7 %copy-start.6 = (bf16[8,24,24,192]{3,2,1,0:T(8,128)(2,1)S(1)}, bf16[8,24,24,192]{3,2,1,0:T(8,128)(2,1)}, u32[]{:S(2)}) copy-start(bf16[8,24,24,192]{3,2,1,0:T(8,128)(2,1)} %param.5) | copy-start | bytes 5308420
  2.0 5.7 %copy-start.7 = (bf16[8,24,24,192]{3,2,1,0:T(8,128)(2,1)S(1)}, bf16[8,24,24,192]{3,2,1,0:T(8,128)(2,1)}, u32[]{:S(2)}) copy-start(bf16[8,24,24,192]{3,2,1,0:T(8,128)(2,1)} %param.6) | copy-start | bytes 5308420
  2.0 12.9 %collective-permute-start = (bf16[8,24,8,192]{3,2,1,0:T(8,128)(2,1)S(1)}, bf16[8,24,8,192]{3,2,1,0:T(8,128)(2,1)S(1)}, u32[]{:S(2)}, u32[]{:S(2)}) collective-permute-start(bf16[8,24,8,192]{3,2,1,0:T(8,128)(2,1)S(1)} %slice.47), channel_id=1, source_target_pairs={{4,0},{8,4},{12,8},{16,12},{20,16},{24,20},{28,24},{0,28},{5,1},{9... | collective-permute-start | bytes 1769480 | tf_op jit(solution)/shard_map/ppermute | solution.py:28
  6.6 16.7 %collective-permute-start.2 = (bf16[8,24,8,192]{3,2,1,0:T(8,128)(2,1)S(1)}, bf16[8,24,8,192]{3,2,1,0:T(8,128)(2,1)S(1)}, u32[]{:S(2)}, u32[]{:S(2)}) collective-permute-start(bf16[8,24,8,192]{3,2,1,0:T(8,128)(2,1)S(1)} %slice.50), channel_id=1, source_target_pairs={{4,0},{8,4},{12,8},{16,12},{20,16},{24,20},{28,24},{0,28},{5,1},{9... | collective-permute-start | bytes 1769480 | tf_op jit(solution)/shard_map/ppermute | solution.py:28
  15.0 9.2 %copy-start.5 = (bf16[8,24,32,192]{3,2,1,0:T(8,128)(2,1)}, bf16[8,24,32,192]{3,2,1,0:T(8,128)(2,1)S(1)}, u32[]{:S(2)}) copy-start(bf16[8,24,32,192]{3,2,1,0:T(8,128)(2,1)S(1)} %constant_dynamic-update-slice_fusion) | copy-start | bytes 7077892
  15.9 31.6 %collective-permute-start.1 = (bf16[8,3,32,192]{3,2,1,0:T(8,128)(2,1)}, bf16[8,3,32,192]{3,2,1,0:T(8,128)(2,1)}, u32[]{:S(2)}, u32[]{:S(2)}) collective-permute-start(bf16[8,3,32,192]{3,2,1,0:T(8,128)(2,1)} %slice.63), channel_id=1, source_target_pairs={{1,0},{2,1},{3,2},{5,4},{6,5},{7,6},{9,8},{10,9},{11,10},{13,12},{... | collective-permute-start | bytes 884744 | tf_op jit(solution)/shard_map/ppermute | solution.py:34
  24.2 26.4 %collective-permute-start.3 = (bf16[8,3,32,192]{3,2,1,0:T(8,128)(2,1)}, bf16[8,3,32,192]{3,2,1,0:T(8,128)(2,1)}, u32[]{:S(2)}, u32[]{:S(2)}) collective-permute-start(bf16[8,3,32,192]{3,2,1,0:T(8,128)(2,1)} %slice.65), channel_id=1, source_target_pairs={{1,0},{2,1},{3,2},{5,4},{6,5},{7,6},{9,8},{10,9},{11,10},{13,12},{... | collective-permute-start | bytes 884744 | tf_op jit(solution)/shard_map/ppermute | solution.py:34
  50.6 3.3 %copy-start = (bf16[192,576]{1,0:T(8,128)(2,1)S(1)}, bf16[192,576]{1,0:T(8,128)(2,1)}, u32[]{:S(2)}) copy-start(bf16[192,576]{1,0:T(8,128)(2,1)} %wqkv_ref.1) | copy-start | bytes 663556
  50.6 3.3 %copy-start.1 = (bf16[192,192]{1,0:T(8,128)(2,1)S(1)}, bf16[192,192]{1,0:T(8,128)(2,1)}, u32[]{:S(2)}) copy-start(bf16[192,192]{1,0:T(8,128)(2,1)} %wproj_ref.1) | copy-start | bytes 221188
  153.0 2.5 copy-start.3
  154.2 85.9 %collective-permute-start.4 = (bf16[8,24,8,192]{3,2,1,0:T(8,128)(2,1)}, bf16[8,24,8,192]{3,2,1,0:T(8,128)(2,1)}, u32[]{:S(2)}, u32[]{:S(2)}) collective-permute-start(bf16[8,24,8,192]{3,2,1,0:T(8,128)(2,1)} %pad_maximum_fusion.3), channel_id=1, source_target_pairs={{28,0},{0,4},{4,8},{8,12},{12,16},{16,20},{20,24},{24,28},{29,1},{... | collective-permute-start | bytes 1769480 | tf_op jit(solution)/shard_map/ppermute | solution.py:28
  222.1 2.0 copy-start.2
  240.1 8.4 %copy-start.4 = (f32[16,6,20736]{2,1,0:T(8,128)S(1)}, f32[16,6,20736]{2,1,0:T(8,128)}, u32[]{:S(2)}) copy-start(f32[16,6,20736]{2,1,0:T(8,128)} %shard_map.86) | copy-start | bytes 23887876
  242.3 12.1 %collective-permute-start.5 = (bf16[8,3,24,192]{3,2,1,0:T(8,128)(2,1)S(1)}, bf16[8,3,24,192]{3,2,1,0:T(8,128)(2,1)S(1)}, u32[]{:S(2)}, u32[]{:S(2)}) collective-permute-start(bf16[8,3,24,192]{3,2,1,0:T(8,128)(2,1)S(1)} %slice.66), channel_id=1, source_target_pairs={{0,1},{1,2},{2,3},{4,5},{5,6},{6,7},{8,9},{9,10},{10,11},{12,13},{... | collective-permute-start | bytes 663560 | tf_op jit(solution)/shard_map/ppermute | solution.py:34
